TPU v7x, 32 devices: a whole 2x2x4 slice. The times are simulated.
32 devices in a mesh: dp: 8 (over y, x, core), expert: 4 (over z).
Axes of the slice: x: 2, y: 2, z: 4, core: 2. Of those that a mesh axis runs over, the one named last changes fastest.
Arguments:
- images: bfloat16 [2, 32, 197, 512], P(None, ('dp', 'expert')), may hold values from -6 to 6
- cotangent: bfloat16 [2, 32, 197, 512], P(None, ('dp', 'expert')), may hold values from -6 to 6
- gates: float32 [2, 32, 197, 2], P(None, ('dp', 'expert')), may hold values from 0.2 to 1
- routes: int32 [2, 32, 197, 2], P(None, ('dp', 'expert')), may hold values from 0 to 3, as said below
- slots: int32 [2, 32, 197, 2], P(None, ('dp', 'expert')), may hold values from 0 to 196, as said below
- dense_master: float32 [2048, 512], P('dp')
- dense_momentum: float32 [2048, 512], P('dp'), may hold values from -256 to 256
- norm_master: float32 [4, 512], P(None, 'dp')
- norm_momentum: float32 [4, 512], P(None, 'dp'), may hold values from -320 to 320
- expert_master: float32 [4, 2, 2048, 512], P('expert', None, 'dp')
- expert_momentum: float32 [4, 2, 2048, 512], P('expert', None, 'dp'), may hold values from -128 to 128
Outputs:
- activations: bfloat16 [2, 32, 197, 512], P(None, ('dp', 'expert'))
- input_grad: bfloat16 [2, 32, 197, 512], P(None, ('dp', 'expert'))
- dense_grad: float32 [2048, 512], P('dp')
- norm_grad: float32 [4, 512], P(None, 'dp')
- expert_grad: float32 [4, 2, 2048, 512], P('expert', None, 'dp')
- dense_moment: float32 [2048, 512], P('dp')
- norm_moment: float32 [4, 512], P(None, 'dp')
- expert_moment: float32 [4, 2, 2048, 512], P('expert', None, 'dp')
- dense_new: float32 [2048, 512], P('dp')
- norm_new: float32 [4, 512], P(None, 'dp')
- expert_new: float32 [4, 2, 2048, 512], P('expert', None, 'dp')
- dense_copy: bfloat16 [2048, 512], P('dp')
- expert_copy: bfloat16 [4, 2, 2048, 512], P('expert', None, 'dp')
Inputs may be any that keep to these rules, and one draw needn't show every extreme that they name: Within each micro-batch and each block of 1 images, a token's two routes differ and no expert is named by more than 197 routes; every expert is named in every block; in each micro-batch, in every run of 4 consecutive blocks that starts at a multiple of 4, some expert is named exactly 197 times in each block. Within a block, the routes to one expert have the slots 0 to their number minus 1, each once.
All inputs are finite; a program needn't handle non-finite values.
Results may differ from a plain program's by a relative error of at most 0.025.
Values may be sent and summed in bfloat16 or wider, within the bound.
A program may use at most 192 MiB of HBM per device.

v0:
```python
from functools import partial

import jax
import jax.numpy as jnp
from jax import lax
from jax.sharding import PartitionSpec as P

HEADS = 8


HIGH = lax.Precision.HIGHEST
NORM_EPS = 1e-06
ORTHO_EPS = 1e-07
NS_A = 3.4445
NS_B = -4.775
NS_C = 2.0315
DECAY = 0.5
LR_QKV = 0.5
LR_OUT = 1.5
LR_EXPERT = 0.5
LR_VECTOR = 0.05


def for_sending(x):
    return jax.tree.map(lambda a: a.astype(jnp.bfloat16) if a.dtype == jnp.float32 else a, x)


def layer_norm(rows, norm_gain, norm_bias):
    row_mean = jnp.mean(rows, axis=-1, keepdims=True)
    centred = rows - row_mean
    variance = jnp.mean(centred * centred, axis=-1, keepdims=True)
    inverse = lax.rsqrt(variance + NORM_EPS)
    normed = centred * inverse
    return (normed * norm_gain + norm_bias, normed, inverse)


def norm_backward(grad_out, normed, inverse, norm_gain):
    grad_gain = jnp.sum(grad_out * normed, axis=0)
    grad_bias = jnp.sum(grad_out, axis=0)
    scaled = grad_out * norm_gain
    grad_rows = inverse * (
        scaled
        - jnp.mean(scaled, axis=-1, keepdims=True)
        - normed * jnp.mean(scaled * normed, axis=-1, keepdims=True)
    )
    return (grad_rows, grad_gain, grad_bias)


def split_heads(projected, heads):
    images_here, seq, triple = projected.shape
    head_size = triple // (3 * heads)
    parts = projected.reshape(images_here, seq, 3, heads, head_size)
    return (parts[:, :, 0], parts[:, :, 1], parts[:, :, 2], head_size ** (-0.5))


def attention_forward(normed_low, w_qkv, w_out, heads):
    images_here, seq, width = normed_low.shape
    projected = jnp.einsum(
        "bsd,ed->bse", normed_low, w_qkv, preferred_element_type=jnp.float32
    ).astype(jnp.bfloat16)
    query_part, key_part, value_part, score_scale = split_heads(projected, heads)
    scores = (
        jnp.einsum("bqhd,bkhd->bhqk", query_part, key_part, preferred_element_type=jnp.float32)
        * score_scale
    )
    top = jnp.max(scores, axis=-1, keepdims=True)
    expo = jnp.exp(scores - top)
    total = jnp.sum(expo, axis=-1, keepdims=True)
    soft_weights = expo / total
    log_total = top + jnp.log(total)
    mixed = jnp.einsum(
        "bhqk,bkhd->bqhd",
        soft_weights.astype(jnp.bfloat16),
        value_part,
        preferred_element_type=jnp.float32,
    )
    mixed = mixed.astype(jnp.bfloat16).reshape(images_here, seq, width)
    branch = jnp.einsum("bsd,ed->bse", mixed, w_out, preferred_element_type=jnp.float32)
    return (branch, (projected, log_total, mixed))


def attention_backward(grad_branch, normed_low, w_qkv, w_out, kept, heads):
    projected, log_total, mixed = kept
    images_here, seq, width = normed_low.shape
    query_part, key_part, value_part, score_scale = split_heads(projected, heads)
    grad_low = grad_branch.astype(jnp.bfloat16)
    grad_out_w = jnp.einsum("bse,bsd->ed", grad_low, mixed, preferred_element_type=jnp.float32)
    grad_mixed = jnp.einsum(
        "bse,ed->bsd", grad_low, w_out, preferred_element_type=jnp.float32
    ).astype(jnp.bfloat16)
    grad_mixed = grad_mixed.reshape(query_part.shape)
    scores = (
        jnp.einsum("bqhd,bkhd->bhqk", query_part, key_part, preferred_element_type=jnp.float32)
        * score_scale
    )
    soft_weights = jnp.exp(scores - log_total)
    soft_low = soft_weights.astype(jnp.bfloat16)
    grad_soft = jnp.einsum(
        "bqhd,bkhd->bhqk", grad_mixed, value_part, preferred_element_type=jnp.float32
    )
    grad_scores = (
        soft_weights * (grad_soft - jnp.sum(soft_weights * grad_soft, axis=-1, keepdims=True))
    ).astype(jnp.bfloat16)
    grad_query = (
        jnp.einsum("bhqk,bkhd->bqhd", grad_scores, key_part, preferred_element_type=jnp.float32)
        * score_scale
    )
    grad_key = (
        jnp.einsum("bhqk,bqhd->bkhd", grad_scores, query_part, preferred_element_type=jnp.float32)
        * score_scale
    )
    grad_value = jnp.einsum(
        "bhqk,bqhd->bkhd", soft_low, grad_mixed, preferred_element_type=jnp.float32
    )
    grad_projected = (
        jnp.stack([grad_query, grad_key, grad_value], axis=2)
        .reshape(images_here, seq, 3 * width)
        .astype(jnp.bfloat16)
    )
    grad_qkv_w = jnp.einsum(
        "bse,bsd->ed", grad_projected, normed_low, preferred_element_type=jnp.float32
    )
    grad_normed = jnp.einsum(
        "bse,ed->bsd", grad_projected, w_qkv, preferred_element_type=jnp.float32
    )
    return (grad_normed, grad_qkv_w, grad_out_w)


def orthogonalize(moment):
    current = moment / (jnp.sqrt(jnp.sum(moment * moment)) + ORTHO_EPS)
    for turn in range(5):
        gram = jnp.einsum("nd,ne->de", current, current, precision=HIGH)
        blend = NS_B * gram + NS_C * jnp.einsum("de,ef->df", gram, gram, precision=HIGH)
        current = NS_A * current + jnp.einsum("nd,de->ne", current, blend, precision=HIGH)
    return current


def shards(
    images,
    cotangent,
    gates,
    routes,
    slots,
    dense_master,
    dense_momentum,
    norm_master,
    norm_momentum,
    expert_master,
    expert_momentum,
):
    micro_count, images_here, seq, width = images.shape
    experts = lax.axis_size("expert")
    dp_count = lax.axis_size("dp")
    rows_dev = images_here * seq
    capacity = min(rows_dev, 4 * rows_dev // experts)
    slot_total = experts * capacity
    tokens_all = micro_count * rows_dev * dp_count * experts
    whole_experts = lax.all_gather(expert_master.astype(jnp.bfloat16), "dp", axis=2, tiled=True)
    w_up = whole_experts[0, 0]
    w_down = whole_experts[0, 1]
    dense_low = dense_master.astype(jnp.bfloat16)
    norm_low = norm_master.astype(jnp.bfloat16)
    grad_dense = jnp.zeros((4 * width, width), jnp.float32)
    grad_norm = jnp.zeros((4, width), jnp.float32)
    grad_up = jnp.zeros(w_up.shape, jnp.float32)
    grad_down = jnp.zeros(w_down.shape, jnp.float32)
    outputs_list = []
    input_list = []
    for micro in range(micro_count):
        dense_whole, norm_whole = (
            lax.all_gather(dense_low, "dp", axis=0, tiled=True),
            lax.all_gather(norm_low, "dp", axis=1, tiled=True),
        )
        norm_wide = norm_whole.astype(jnp.float32)
        block = images[micro].astype(jnp.float32).reshape(rows_dev, width)
        normed_full, normed_one, inverse_one = layer_norm(block, norm_wide[0], norm_wide[1])
        normed_one_low = normed_full.astype(jnp.bfloat16).reshape(images_here, seq, width)
        branch, kept = attention_forward(
            normed_one_low, dense_whole[: 3 * width], dense_whole[3 * width :], HEADS
        )
        residual = block + branch.reshape(rows_dev, width)
        normed_two_full, normed_two, inverse_two = layer_norm(residual, norm_wide[2], norm_wide[3])
        normed_two_low = normed_two_full.astype(jnp.bfloat16)
        index = (routes[micro] * capacity + slots[micro]).reshape(rows_dev, 2)
        gate_pair = gates[micro].reshape(rows_dev, 2)
        picks = jnp.arange(slot_total)[:, None, None] == index[None, :, :]
        dispatch = jnp.sum(picks.astype(jnp.int32), axis=2).astype(jnp.bfloat16)
        send = jnp.dot(dispatch, normed_two_low, preferred_element_type=jnp.float32).astype(
            jnp.bfloat16
        )
        received = lax.all_to_all(
            send.reshape(experts, capacity, width),
            "expert",
            split_axis=0,
            concat_axis=0,
            tiled=True,
        )
        sources, count, features = received.shape
        rows_in = received.reshape(sources * count, features)
        pre = jnp.einsum("rd,fd->rf", rows_in, w_up, preferred_element_type=jnp.float32)
        hidden = jax.nn.gelu(pre, approximate=False).astype(jnp.bfloat16)
        produced = jnp.dot(hidden, w_down, preferred_element_type=jnp.float32).astype(jnp.bfloat16)
        returned = lax.all_to_all(
            produced.reshape(sources, count, features),
            "expert",
            split_axis=0,
            concat_axis=0,
            tiled=True,
        )
        returned, received, pre = (returned, received, pre.reshape(sources, count, pre.shape[1]))
        back_flat = returned.reshape(slot_total, width)
        taken = back_flat[index].astype(jnp.float32)
        moe = gate_pair[:, 0:1] * taken[:, 0] + gate_pair[:, 1:2] * taken[:, 1]
        outputs_list.append((residual + moe).astype(jnp.bfloat16).reshape(images_here, seq, width))
        grad_output = cotangent[micro].astype(jnp.float32).reshape(rows_dev, width)
        spread = jnp.sum(jnp.where(picks, gate_pair[None, :, :], 0.0), axis=2)
        grad_send = jnp.dot(spread, grad_output, precision=HIGH).astype(jnp.bfloat16)
        grad_received = lax.all_to_all(
            grad_send.reshape(experts, capacity, width),
            "expert",
            split_axis=0,
            concat_axis=0,
            tiled=True,
        )
        grad_rows_out = grad_received.reshape(slot_total, width)
        pre_rows = pre.reshape(slot_total, pre.shape[2])
        hidden_full, gelu_pull = jax.vjp(partial(jax.nn.gelu, approximate=False), pre_rows)
        hidden = hidden_full.astype(jnp.bfloat16)
        grad_down = grad_down + jnp.einsum(
            "rf,rd->fd", hidden, grad_rows_out, preferred_element_type=jnp.float32
        )
        grad_hidden = jnp.einsum(
            "rd,fd->rf", grad_rows_out, w_down, preferred_element_type=jnp.float32
        )
        grad_pre = gelu_pull(grad_hidden)[0].astype(jnp.bfloat16)
        rows_in = received.reshape(slot_total, width)
        grad_up = grad_up + jnp.einsum(
            "rf,rd->fd", grad_pre, rows_in, preferred_element_type=jnp.float32
        )
        grad_in = jnp.dot(grad_pre, w_up, preferred_element_type=jnp.float32).astype(jnp.bfloat16)
        grad_back = lax.all_to_all(
            grad_in.reshape(experts, capacity, width),
            "expert",
            split_axis=0,
            concat_axis=0,
            tiled=True,
        )
        pair_back = grad_back.reshape(slot_total, width)[index].astype(jnp.float32)
        grad_normed_two = pair_back[:, 0] + pair_back[:, 1]
        grad_two_rows, gain_two_grad, bias_two_grad = norm_backward(
            grad_normed_two, normed_two, inverse_two, norm_wide[2]
        )
        grad_residual = grad_output + grad_two_rows
        dense_again, norm_again = (
            lax.all_gather(dense_low, "dp", axis=0, tiled=True),
            lax.all_gather(norm_low, "dp", axis=1, tiled=True),
        )
        norm_again_wide = norm_again.astype(jnp.float32)
        grad_normed_one, grad_qkv_w, grad_out_w = attention_backward(
            grad_residual.reshape(images_here, seq, width),
            normed_one_low,
            dense_again[: 3 * width],
            dense_again[3 * width :],
            kept,
            HEADS,
        )
        grad_one_rows, gain_one_grad, bias_one_grad = norm_backward(
            grad_normed_one.reshape(rows_dev, width), normed_one, inverse_one, norm_again_wide[0]
        )
        input_list.append(
            (grad_residual + grad_one_rows).astype(jnp.bfloat16).reshape(images_here, seq, width)
        )
        grad_dense = grad_dense + jnp.concatenate([grad_qkv_w, grad_out_w], axis=0)
        grad_norm = grad_norm + jnp.stack(
            [gain_one_grad, bias_one_grad, gain_two_grad, bias_two_grad]
        )
    expert_terms = jnp.stack([grad_up, grad_down])[None]
    summed_dense, summed_norm, expert_grad = (
        lax.psum_scatter(
            grad_dense.astype(jnp.bfloat16), "dp", scatter_dimension=0, tiled=True
        ).astype(jnp.float32),
        lax.psum_scatter(
            grad_norm.astype(jnp.bfloat16), "dp", scatter_dimension=1, tiled=True
        ).astype(jnp.float32),
        lax.psum_scatter(
            expert_terms.astype(jnp.bfloat16), "dp", scatter_dimension=2, tiled=True
        ).astype(jnp.float32),
    )
    dense_grad, norm_grad = (
        lax.psum(summed_dense.astype(jnp.bfloat16), "expert").astype(jnp.float32),
        lax.psum(summed_norm.astype(jnp.bfloat16), "expert").astype(jnp.float32),
    )
    dense_moment = DECAY * dense_momentum + dense_grad
    norm_moment = DECAY * norm_momentum + norm_grad
    expert_moment = DECAY * expert_momentum + expert_grad
    row_start = lax.axis_index("dp")
    dense_rows = dense_master.shape[0]
    hidden_rows = expert_master.shape[2]
    slot_ids = jnp.arange(dp_count)
    dense_owner = jnp.where(row_start * dense_rows >= 3 * width, 3, 2)
    dense_send = jnp.where((slot_ids == dense_owner)[:, None, None], dense_moment[None], 0.0)
    expert_pick = slot_ids[:, None] == jnp.arange(2)[None, :]
    expert_send = jnp.where(expert_pick[:, :, None, None], expert_moment[0][None], 0.0)
    dense_got, expert_got = (
        lax.all_to_all(
            dense_send.astype(jnp.bfloat16), "dp", split_axis=0, concat_axis=0, tiled=True
        ).astype(dense_send.dtype),
        lax.all_to_all(
            expert_send.astype(jnp.bfloat16), "dp", split_axis=0, concat_axis=0, tiled=True
        ).astype(expert_send.dtype),
    )
    dense_gathered = dense_got.reshape(dp_count * dense_rows, width)
    expert_gathered = expert_got.transpose(1, 0, 2, 3).reshape(2, dp_count * hidden_rows, width)
    dense_zero = jnp.zeros((dp_count * dense_rows, width), jnp.float32)
    expert_zero = jnp.zeros((2, dp_count * hidden_rows, width), jnp.float32)

    def own_upper():
        return (dense_zero, expert_zero.at[0].set(orthogonalize(expert_gathered[0])))

    def own_lower():
        return (dense_zero, expert_zero.at[1].set(orthogonalize(expert_gathered[1])))

    def own_query():
        return (
            dense_zero.at[: 3 * width].set(LR_QKV * orthogonalize(dense_gathered[: 3 * width])),
            expert_zero,
        )

    def own_output():
        return (
            dense_zero.at[3 * width :].set(LR_OUT * orthogonalize(dense_gathered[3 * width :])),
            expert_zero,
        )

    def own_nothing():
        return (dense_zero, expert_zero)

    dense_dir, expert_dir = lax.switch(
        jnp.minimum(row_start, 4), [own_upper, own_lower, own_query, own_output, own_nothing]
    )
    dense_back = dense_dir.reshape(dp_count, dense_rows, width)
    expert_back = expert_dir.reshape(2, dp_count, hidden_rows, width).transpose(1, 0, 2, 3)
    dense_ret, expert_ret = (
        lax.all_to_all(
            for_sending(dense_back), "dp", split_axis=0, concat_axis=0, tiled=True
        ).astype(dense_back.dtype),
        lax.all_to_all(
            for_sending(expert_back), "dp", split_axis=0, concat_axis=0, tiled=True
        ).astype(expert_back.dtype),
    )
    dense_step = jnp.sum(dense_ret, axis=0)
    expert_shard = jnp.sum(expert_ret, axis=0)[None]
    dense_new = dense_master - dense_step
    norm_new = norm_master - LR_VECTOR * tokens_all ** (-0.5) * norm_moment
    expert_new = expert_master - LR_EXPERT * expert_shard
    return (
        jnp.stack(outputs_list),
        jnp.stack(input_list),
        dense_grad,
        norm_grad,
        expert_grad,
        dense_moment,
        norm_moment,
        expert_moment,
        dense_new,
        norm_new,
        expert_new,
        dense_new.astype(jnp.bfloat16),
        expert_new.astype(jnp.bfloat16),
    )


def solution(mesh):
    in_specs = (
        P(None, ("dp", "expert"), None, None),
        P(None, ("dp", "expert"), None, None),
        P(None, ("dp", "expert"), None, None),
        P(None, ("dp", "expert"), None, None),
        P(None, ("dp", "expert"), None, None),
        P("dp", None),
        P("dp", None),
        P(None, "dp"),
        P(None, "dp"),
        P("expert", None, "dp", None),
        P("expert", None, "dp", None),
    )
    out_specs = (
        P(None, ("dp", "expert"), None, None),
        P(None, ("dp", "expert"), None, None),
        P("dp", None),
        P(None, "dp"),
        P("expert", None, "dp", None),
        P("dp", None),
        P(None, "dp"),
        P("expert", None, "dp", None),
        P("dp", None),
        P(None, "dp"),
        P("expert", None, "dp", None),
        P("dp", None),
        P("expert", None, "dp", None),
    )
    return jax.shard_map(shards, mesh=mesh, in_specs=in_specs, out_specs=out_specs, check_vma=False)
```

profile of v0, /device:TPU:5, one launch (start us, length us, event | category | flops | bytes accessed | tf_op | source)
XLA Modules:
  0.0 698.7 jit_solution(15484559897462669001)
XLA Ops:
  12.7 7.3 %select_reduce_fusion.1 = f32[788,197]{0,1:T(8,128)S(1)} fusion(f32[197,2]{1,0:T(8,128)S(1)} %copy.232, s32[197,2]{1,0:T(8,128)S(1)} %copy.220), kind=kLoop, calls=%fused_computation.151 | loop fusion | flops 776180 | bytes 624096 | tf_op jit(solution)/shard_map/reduce_sum | solution.py:216
  22.1 4.6 all-to-all-start.4
  27.6 9.9 %all-gather = bf16[8,64,4]{1,2,0:T(4,128)(2,1)S(1)} all-gather(bf16[1,64,4]{1,2,0:T(4,128)(2,1)S(1)} %convert_bitcast_fusion.3), channel_id=1, replica_groups=mesh['dp'=8,'expert'=4] {'dp'}, dimensions={0}, use_global_device_ids=true | all-gather | bytes 4608 | tf_op jit(solution)/shard_map/all_gather | solution.py:172
  40.6 7.5 %select_reduce_fusion = f32[788,197]{0,1:T(8,128)S(1)} fusion(f32[197,2]{1,0:T(8,128)S(1)} %copy.240, s32[197,2]{1,0:T(8,128)S(1)} %copy.227), kind=kLoop, calls=%fused_computation.150 | loop fusion | flops 776180 | bytes 624096 | tf_op jit(solution)/shard_map/reduce_sum | solution.py:216
  69.1 5.6 all-to-all-start.6
  78.4 16.8 %all-to-all-done.6 = bf16[4,197,512]{2,1,0:T(8,128)(2,1)} async-done(((bf16[4,197,512]{2,1,0:T(8,128)(2,1)}), bf16[4,197,512]{2,1,0:T(8,128)(2,1)}, u32[]{:S(2)}, u32[]{:S(2)}) %all-to-all-start.6) | async-done | bytes 806944 | tf_op jit(solution)/shard_map/all_to_all | solution.py:218
  104.6 15.3 %all-to-all-done = bf16[4,197,512]{2,1,0:T(8,128)(2,1)} async-done(((bf16[4,197,512]{2,1,0:T(8,128)(2,1)}), bf16[4,197,512]{2,1,0:T(8,128)(2,1)}, u32[]{:S(2)}, u32[]{:S(2)}) %all-to-all-start) | async-done | bytes 806944 | tf_op jit(solution)/shard_map/all_to_all | solution.py:191
  127.0 16.7 %all-to-all-done.2 = bf16[4,197,512]{2,1,0:T(8,128)(2,1)S(1)} async-done(((bf16[4,197,512]{2,1,0:T(8,128)(2,1)}), bf16[4,197,512]{2,1,0:T(8,128)(2,1)S(1)}, u32[]{:S(2)}, u32[]{:S(2)}) %all-to-all-start.2) | async-done | bytes 806944 | tf_op jit(solution)/shard_map/all_to_all | solution.py:191
  144.8 17.7 %multiply_convert_fusion = (bf16[788,2048]{1,0:T(8,128)(2,1)}, f32[788,2048]{1,0:T(8,128)S(1)}, f32[788,2048]{1,0:T(8,128)S(1)}) fusion(bf16[788,512]{1,0:T(8,128)(2,1)} %reshape.1345, bf16[1,2,2048,512]{3,2,1,0:T(8,128)(2,1)} %all-gather.6.cloned.1.call-done), kind=kOutput, calls=%fused_computation.93 | convolution fusion | flops 1757454336 | bytes 19046400 | tf_op jit(solution)/shard_map/rd,fd->rf/dot_general | solution.py:200
  174.5 17.5 %multiply_convert_fusion.1 = (bf16[788,2048]{1,0:T(8,128)(2,1)}, f32[788,2048]{1,0:T(8,128)S(1)}, f32[788,2048]{1,0:T(8,128)S(1)}) fusion(bf16[788,512]{1,0:T(8,128)(2,1)S(1)} %reshape.1335, bf16[1,2,2048,512]{3,2,1,0:T(8,128)(2,1)} %all-gather.6.cloned.1.call-done), kind=kOutput, calls=%fused_computation.106 | convolution fusion | flops 1757454336 | bytes 19042304 | tf_op jit(solution)/shard_map/rd,fd->rf/dot_general | solution.py:200
  210.1 15.1 %all-to-all-done.5 = bf16[4,197,512]{2,1,0:T(8,128)(2,1)S(1)} async-done(((bf16[4,197,512]{2,1,0:T(8,128)(2,1)}), bf16[4,197,512]{2,1,0:T(8,128)(2,1)S(1)}, u32[]{:S(2)}, u32[]{:S(2)}) %all-to-all-start.5) | async-done | bytes 806944 | tf_op jit(solution)/shard_map/all_to_all | solution.py:241
  265.0 26.2 %reduce-scatter.6.cloned.1.call-done = bf16[256,512]{1,0:T(8,128)(2,1)} async-done(((bf16[2048,512]{1,0:T(8,128)(2,1)}), bf16[256,512]{1,0:T(8,128)(2,1)}) %reduce-scatter.6.cloned.1.call-update) | async-done | bytes 262160 | tf_op jit(solution)/shard_map/reduce_scatter | solution.py:279
  305.2 26.1 %all-reduce.6.cloned.1.call-done = bf16[256,512]{1,0:T(8,128)(2,1)} async-done(((bf16[256,512]{1,0:T(8,128)(2,1)}), bf16[256,512]{1,0:T(8,128)(2,1)}) %all-reduce.6.cloned.1.call-update) | async-done | bytes 262160 | tf_op jit(solution)/shard_map/psum | solution.py:290
  336.5 6.4 all-to-all-start.9
  343.0 51.0 %reduce-scatter.8.cloned.1.call-done = bf16[1,2,256,512]{3,2,1,0:T(8,128)(2,1)} async-done(((bf16[1,2,2048,512]{3,2,1,0:T(8,128)(2,1)}), bf16[1,2,256,512]{3,2,1,0:T(8,128)(2,1)}) %reduce-scatter.8.cloned.1.call-update) | async-done | bytes 524304 | tf_op jit(solution)/shard_map/reduce_scatter | solution.py:285
  400.1 5.5 all-to-all-start.8
  411.2 39.7 %all-to-all-done.8 = bf16[8,2,256,512]{3,2,1,0:T(8,128)(2,1)} async-done(((bf16[8,2,256,512]{3,2,1,0:T(8,128)(2,1)}), bf16[8,2,256,512]{3,2,1,0:T(8,128)(2,1)}, u32[]{:S(2)}, u32[]{:S(2)}) %all-to-all-start.8) | async-done | bytes 4194336 | tf_op jit(solution)/shard_map/all_to_all | solution.py:308
  461.2 42.7 %conditional.1 = (bf16[2048,512]{1,0:T(8,128)(2,1)S(1)}, bf16[2,2048,512]{2,1,0:T(8,128)(2,1)}) conditional(s32[]{:T(128)} %clamp.3, f32[2,8,256,512]{3,2,0,1:T(8,128)S(1)} %convert_bitcast_fusion, f32[2,8,256,512]{3,2,0,1:T(8,128)S(1)} %convert_bitcast_fusion, f32[8,256,512]{2,1,0:T(8,128)} %convert_element_type.431, ...), branch_computations={%region_39.41_spmd, %region_41.43_spmd, %region_43.45_spmd, %regio... | conditional | flops 72496185344 | bytes 136314960 | solution.py:338
  505.2 89.0 %all-to-all-start.10 = ((bf16[8,256,512]{2,1,0:T(8,128)(2,1)}), bf16[8,256,512]{2,1,0:T(8,128)(2,1)S(1)}, u32[]{:S(2)}, u32[]{:S(2)}) async-start(bf16[8,256,512]{2,1,0:T(8,128)(2,1)} %bitcast.503), calls=%async_computation.12 | async-start | bytes 4194304 | tf_op jit(solution)/shard_map/all_to_all | solution.py:344
  607.5 4.5 copy.249
  612.0 5.0 all-to-all-done.10
  617.0 8.3 %all-to-all-start.11 = ((bf16[8,2,256,512]{3,2,1,0:T(8,128)(2,1)}), bf16[8,2,256,512]{3,2,1,0:T(8,128)(2,1)}, u32[]{:S(2)}, u32[]{:S(2)}) async-start(bf16[8,2,256,512]{3,2,1,0:T(8,128)(2,1)} %copy.249), calls=%async_computation.13 | async-start | bytes 8388608 | tf_op jit(solution)/shard_map/all_to_all | solution.py:347
  639.3 33.6 %reduce-scatter.10.cloned.1.call-done = bf16[64,4]{1,0:T(8,128)(2,1)} async-done(((bf16[512,4]{1,0:T(8,128)(2,1)}), bf16[64,4]{1,0:T(8,128)(2,1)}) %reduce-scatter.10.cloned.1.call-update) | async-done | bytes 528
  673.7 9.6 %psum.15 = bf16[4,64]{1,0:T(4,128)(2,1)S(1)} all-reduce(bf16[4,64]{1,0:T(4,128)(2,1)S(1)} %copy.265), channel_id=1, replica_groups=mesh['dp'=8,'expert'=4] {'expert'}, use_global_device_ids=true, to_apply=%region_37.38 | all-reduce | flops 256 | bytes 1024 | tf_op jit(solution)/shard_map/psum | solution.py:291
  (402 shorter events, 203.0 us)
Async XLA Ops:
  7.2 50.4 %all-gather.4.cloned.1.call-start = ((), (), s32[]{:S(2)}) async-start(), calls=%async_computation.15 | async-start | bytes 2359296 | tf_op jit(solution)/shard_map/all_gather | solution.py:171
  22.1 47.0 %all-to-all-start.4 = ((bf16[4,197,512]{2,1,0:T(8,128)(2,1)}), bf16[4,197,512]{2,1,0:T(8,128)(2,1)S(1)}, u32[]{:S(2)}, u32[]{:S(2)}) async-start(bf16[4,197,512]{2,1,0:T(8,128)(2,1)} %reshape.1348), calls=%async_computation.4 | async-start | bytes 1638400 | tf_op jit(solution)/shard_map/all_to_all | solution.py:218
  26.7 118.2 %all-gather.6.cloned.1.call-start = ((), (), s32[]{:S(2)}) async-start(), calls=%async_computation.16 | async-start | bytes 4718592 | tf_op jit(solution)/shard_map/all_gather | solution.py:158
  69.1 26.2 %all-to-all-start.6 = ((bf16[4,197,512]{2,1,0:T(8,128)(2,1)}), bf16[4,197,512]{2,1,0:T(8,128)(2,1)}, u32[]{:S(2)}, u32[]{:S(2)}) async-start(bf16[4,197,512]{2,1,0:T(8,128)(2,1)} %reshape.1353), calls=%async_computation.6 | async-start | bytes 1638400 | tf_op jit(solution)/shard_map/all_to_all | solution.py:218
  95.2 24.6 %all-to-all-start = ((bf16[4,197,512]{2,1,0:T(8,128)(2,1)}), bf16[4,197,512]{2,1,0:T(8,128)(2,1)}, u32[]{:S(2)}, u32[]{:S(2)}) async-start(bf16[4,197,512]{2,1,0:T(8,128)(2,1)} %reshape.1334), calls=%async_computation | async-start | bytes 1638400 | tf_op jit(solution)/shard_map/all_to_all | solution.py:191
  119.9 23.8 %all-to-all-start.2 = ((bf16[4,197,512]{2,1,0:T(8,128)(2,1)}), bf16[4,197,512]{2,1,0:T(8,128)(2,1)S(1)}, u32[]{:S(2)}, u32[]{:S(2)}) async-start(bf16[4,197,512]{2,1,0:T(8,128)(2,1)} %reshape.1344), calls=%async_computation.2 | async-start | bytes 1638400 | tf_op jit(solution)/shard_map/all_to_all | solution.py:191
  123.6 68.4 %copy-start.52 = (bf16[788,512]{1,0:T(8,128)(2,1)}, bf16[788,512]{1,0:T(8,128)(2,1)S(1)}, u32[]{:S(2)}) copy-start(bf16[788,512]{1,0:T(8,128)(2,1)S(1)} %reshape.1349) | copy-start | bytes 2420740
  170.8 29.5 %all-to-all-start.7 = ((bf16[4,197,512]{2,1,0:T(8,128)(2,1)}), bf16[4,197,512]{2,1,0:T(8,128)(2,1)S(1)}, u32[]{:S(2)}, u32[]{:S(2)}) async-start(bf16[4,197,512]{2,1,0:T(8,128)(2,1)} %reshape.1355), calls=%async_computation.7 | async-start | bytes 1638400 | tf_op jit(solution)/shard_map/all_to_all | solution.py:241
  200.4 24.9 %all-to-all-start.5 = ((bf16[4,197,512]{2,1,0:T(8,128)(2,1)}), bf16[4,197,512]{2,1,0:T(8,128)(2,1)S(1)}, u32[]{:S(2)}, u32[]{:S(2)}) async-start(bf16[4,197,512]{2,1,0:T(8,128)(2,1)} %reshape.1350), calls=%async_computation.5 | async-start | bytes 1638400 | tf_op jit(solution)/shard_map/all_to_all | solution.py:241
  204.9 86.3 %reduce-scatter.6.cloned.1.call-start = ((), (), s32[]{:S(2)}) async-start(), calls=%async_computation.17 | async-start | bytes 2359296 | tf_op jit(solution)/shard_map/reduce_scatter | solution.py:279
  251.3 80.0 %all-reduce.6.cloned.1.call-start = ((), (), s32[]{:S(2)}) async-start(), calls=%async_computation.18 | async-start | bytes 524288 | tf_op jit(solution)/shard_map/psum | solution.py:290
  291.2 102.8 %reduce-scatter.8.cloned.1.call-start = ((), (), s32[]{:S(2)}) async-start(), calls=%async_computation.19 | async-start | bytes 4718592 | tf_op jit(solution)/shard_map/reduce_scatter | solution.py:285
  300.9 34.8 %all-to-all-start.3 = ((bf16[4,197,512]{2,1,0:T(8,128)(2,1)}), bf16[4,197,512]{2,1,0:T(8,128)(2,1)S(1)}, u32[]{:S(2)}, u32[]{:S(2)}) async-start(bf16[4,197,512]{2,1,0:T(8,128)(2,1)} %reshape.1346), calls=%async_computation.3 | async-start | bytes 1638400 | tf_op jit(solution)/shard_map/all_to_all | solution.py:203
  305.2 88.8 %copy-start.44 = (f32[1,2,256,512]{3,2,1,0:T(8,128)S(1)}, f32[1,2,256,512]{3,2,1,0:T(8,128)}, u32[]{:S(2)}) copy-start(f32[1,2,256,512]{3,2,1,0:T(8,128)} %param.34) | copy-start | bytes 3145732
  336.5 63.6 %all-to-all-start.9 = ((bf16[8,256,512]{2,1,0:T(8,128)(2,1)}), bf16[8,256,512]{2,1,0:T(8,128)(2,1)S(1)}, u32[]{:S(2)}, u32[]{:S(2)}) async-start(bf16[8,256,512]{2,1,0:T(8,128)(2,1)} %select_convert_fusion.1), calls=%async_computation.11 | async-start | bytes 4194304 | tf_op jit(solution)/shard_map/all_to_all | solution.py:305
  400.1 50.7 %all-to-all-start.8 = ((bf16[8,2,256,512]{3,2,1,0:T(8,128)(2,1)}), bf16[8,2,256,512]{3,2,1,0:T(8,128)(2,1)}, u32[]{:S(2)}, u32[]{:S(2)}) async-start(bf16[8,2,256,512]{3,2,1,0:T(8,128)(2,1)} %select_convert_fusion), calls=%async_computation.10 | async-start | bytes 8388608 | tf_op jit(solution)/shard_map/all_to_all | solution.py:308
  450.9 53.0 %all-to-all-start.1 = ((bf16[4,197,512]{2,1,0:T(8,128)(2,1)}), bf16[4,197,512]{2,1,0:T(8,128)(2,1)}, u32[]{:S(2)}, u32[]{:S(2)}) async-start(bf16[4,197,512]{2,1,0:T(8,128)(2,1)} %reshape.1336), calls=%async_computation.1 | async-start | bytes 1638400 | tf_op jit(solution)/shard_map/all_to_all | solution.py:203
  503.9 90.3 %copy-start.81 = (f32[197,2]{0,1:T(2,128)S(1)}, f32[197,2]{0,1:T(2,128)}, u32[]{:S(2)}) copy-start(f32[197,2]{0,1:T(2,128)} %copy-done.80) | copy-start | bytes 4732
  503.9 90.3 %copy-start.83 = (f32[197,2]{0,1:T(2,128)S(1)}, f32[197,2]{0,1:T(2,128)}, u32[]{:S(2)}) copy-start(f32[197,2]{0,1:T(2,128)} %copy-done.82) | copy-start | bytes 4732
  503.9 92.3 %copy-start.9 = (s32[1024]{0:T(1024)S(1)}, s32[1024]{0:T(1024)}, u32[]{:S(2)}) copy-start(s32[1024]{0:T(1024)} %copy-done.8) | copy-start | bytes 12292
  505.2 111.8 %all-to-all-start.10 = ((bf16[8,256,512]{2,1,0:T(8,128)(2,1)}), bf16[8,256,512]{2,1,0:T(8,128)(2,1)S(1)}, u32[]{:S(2)}, u32[]{:S(2)}) async-start(bf16[8,256,512]{2,1,0:T(8,128)(2,1)} %bitcast.503), calls=%async_computation.12 | async-start | bytes 4194304 | tf_op jit(solution)/shard_map/all_to_all | solution.py:344
  617.0 70.0 %all-to-all-start.11 = ((bf16[8,2,256,512]{3,2,1,0:T(8,128)(2,1)}), bf16[8,2,256,512]{3,2,1,0:T(8,128)(2,1)}, u32[]{:S(2)}, u32[]{:S(2)}) async-start(bf16[8,2,256,512]{3,2,1,0:T(8,128)(2,1)} %copy.249), calls=%async_computation.13 | async-start | bytes 8388608 | tf_op jit(solution)/shard_map/all_to_all | solution.py:347
  625.3 47.6 %reduce-scatter.10.cloned.1.call-start = ((), (), s32[]{:S(2)}) async-start(), calls=%async_computation.20 | async-start | bytes 147456
  634.8 48.6 %copy-start.103 = (f32[4,64]{1,0:T(4,128)S(1)}, f32[4,64]{1,0:T(4,128)}, u32[]{:S(2)}) copy-start(f32[4,64]{1,0:T(4,128)} %param.31) | copy-start | bytes 3076
  (104 other events, 960.4 us)
Sparse Core Ops, SparseCore 0:
  10.4 29.3 all-gather.3
  42.3 36.4 all-gather.5
  251.4 39.7 reduce-scatter.5
  293.4 37.8 all-reduce.5
  334.5 59.4 reduce-scatter.7
  630.6 42.2 reduce-scatter.9
where the time goes:
time: 710 us; the launch traced here: 699 us
  waiting for transfers between devices  246 us (35%)
  starting transfers between devices  144 us (20%)
  matrix products  100 us (14%)
  local copies, waits for them, and re-layouts  66.2 us (9%)
  other arithmetic  65.9 us (9%)
  loops' own time  40.2 us (6%)
  blocking collectives  19.5 us (3%)
  between operations  16.5 us (2%)
    all_to_all x1, starting transfers between devices, shards(): lax.all_to_all(for_sending(dense_back), 'dp', split_axis=0, concat_axis=0...  89 us
    reduce_scatter x1, waiting for transfers between devices, shards(): lax.psum_scatter(expert_terms.astype(jnp.bfloat16), 'dp', scatter_dimensi...  51 us
    another operation x1, loops' own time, shards(): lax.switch(jnp.minimum(row_start, 4), [own_upper, own_lower, own_query, o...  40.2 us
    all_to_all x1, waiting for transfers between devices, shards(): lax.all_to_all(expert_send.astype(jnp.bfloat16), 'dp', split_axis=0, conc...  39.7 us
    dot_general x2, matrix products, shards(): jnp.einsum('rd,fd->rf', rows_in, w_up, preferred_element_type=jnp.float32)  35.3 us
    unnamed x7, waiting for transfers between devices  33.7 us
    all_to_all x2, waiting for transfers between devices, shards(): lax.all_to_all(send.reshape(experts, capacity, width), 'expert', split_ax...  32.1 us
    reduce_scatter x1, waiting for transfers between devices, shards(): lax.psum_scatter(grad_dense.astype(jnp.bfloat16), 'dp', scatter_dimension...  26.2 us
  transfers between devices with their start and end apart: 18, of which 10 were waited for; matrix products, arithmetic and copies ran while one was open for 24% of the time, Pallas kernels for 0%

commit v1 on v0

--- a/solution.py
+++ b/solution.py
@@ -3,7 +3,12 @@
 import jax
 import jax.numpy as jnp
 from jax import lax
+from jax.experimental import pallas as pl
+from jax.experimental.pallas import tpu as pltpu
 from jax.sharding import PartitionSpec as P
+
+MESH = pl.DeviceIdType.MESH
+NT = (((1,), (1,)), ((), ()))
 
 HEADS = 8
 
@@ -19,10 +24,6 @@
 LR_OUT = 1.5
 LR_EXPERT = 0.5
 LR_VECTOR = 0.05
-
-
-def for_sending(x):
-    return jax.tree.map(lambda a: a.astype(jnp.bfloat16) if a.dtype == jnp.float32 else a, x)
 
 
 def layer_norm(rows, norm_gain, norm_bias):
@@ -126,13 +127,228 @@
     return (grad_normed, grad_qkv_w, grad_out_w)
 
 
-def orthogonalize(moment):
-    current = moment / (jnp.sqrt(jnp.sum(moment * moment)) + ORTHO_EPS)
-    for turn in range(5):
-        gram = jnp.einsum("nd,ne->de", current, current, precision=HIGH)
-        blend = NS_B * gram + NS_C * jnp.einsum("de,ef->df", gram, gram, precision=HIGH)
-        current = NS_A * current + jnp.einsum("nd,de->ne", current, blend, precision=HIGH)
-    return current
+def muon_kernel(
+    n_dp, width, expert_grad, dense_grad, expert_momentum, dense_momentum, expert_master,
+    dense_master, expert_moment, dense_moment, expert_new, dense_new, expert_copy, dense_copy,
+    outgoing, held, wide, low, blend, back, send_sem, take_sem, return_sem, back_sem,
+):
+    me = lax.axis_index("dp")
+    rows = dense_grad.shape[0]
+    turned = rows % 128 == 0
+
+    def turn_over(block):
+        return block.T if turned else block
+
+    def slot(ref, place):
+        where = pl.ds(pl.multiple_of(place * rows, rows), rows)
+        return ref.at[:, where] if turned else ref.at[where, :]
+
+    query_devices = 3 * width // rows
+    own_up, own_down, own_query, own_out = 0, 3 * n_dp // 4, n_dp // 4, n_dp // 2
+    dense_owner = jnp.where(me < query_devices, own_query, own_out)
+    dense_place = jnp.where(me < query_devices, me, me - query_devices)
+    barrier = pltpu.get_barrier_semaphore()
+    for step in range(1, n_dp):
+        pl.semaphore_signal(
+            barrier, inc=1, device_id={"dp": lax.rem(me + step, n_dp)}, device_id_type=MESH
+        )
+    for job in range(2):
+        moment = DECAY * expert_momentum[0, job] + expert_grad[0, job]
+        expert_moment[0, job] = moment
+        outgoing[job] = turn_over(moment.astype(jnp.bfloat16))
+    moment = DECAY * dense_momentum[...] + dense_grad[...]
+    dense_moment[...] = moment
+    outgoing[2] = turn_over(moment.astype(jnp.bfloat16))
+    pl.semaphore_wait(barrier, n_dp - 1)
+
+    owners = (own_up, own_down, dense_owner)
+    places = (me, me, dense_place)
+    for job in range(3):
+        @pl.when(me != owners[job])
+        def _():
+            pltpu.make_async_remote_copy(
+                src_ref=outgoing.at[job], dst_ref=slot(held, places[job]),
+                send_sem=send_sem.at[job], recv_sem=take_sem.at[me],
+                device_id={"dp": owners[job]}, device_id_type=MESH,
+            ).start()
+
+        @pl.when(me == owners[job])
+        def _():
+            slot(held, places[job])[...] = outgoing[job]
+
+    def take(source):
+        @pl.when(me != source)
+        def _():
+            pltpu.make_async_remote_copy(
+                src_ref=outgoing.at[0], dst_ref=slot(held, 0),
+                send_sem=send_sem.at[0], recv_sem=take_sem.at[source],
+                device_id={"dp": source}, device_id_type=MESH,
+            ).wait_recv()
+
+    query_rows = 3 * width
+    out_rows = n_dp * rows - query_rows
+    total = n_dp * rows
+
+    def clear(first):
+        zeros = jnp.zeros((total - first, width), jnp.bfloat16)
+        if turned:
+            held[:, first:] = zeros.T
+        else:
+            held[first:, :] = zeros
+
+    def columns(start):
+        where = slice(start, start + width)
+        return (held[:, where] if turned else held[where, :].T).astype(jnp.float32)
+
+    @pl.when((me == own_up) | (me == own_down))
+    def _():
+        for source in range(n_dp):
+            take(source)
+
+    @pl.when(me == own_query)
+    def _():
+        clear(query_rows)
+        for source in range(query_devices):
+            take(source)
+
+    @pl.when(me == own_out)
+    def _():
+        clear(out_rows)
+        for source in range(query_devices, n_dp):
+            take(source)
+
+    owner = (me == own_up) | (me == own_down) | (me == own_query) | (me == own_out)
+
+    @pl.when(owner)
+    def _():
+        square = jnp.zeros((1, 1), jnp.float32)
+        for start in range(0, total, width):
+            part = columns(start)
+            square = square + jnp.sum(part * part, keepdims=True)
+        scale = 1.0 / (jnp.sqrt(square) + ORTHO_EPS)
+        for start in range(0, total, width):
+            part = columns(start) * scale
+            wide[:, start : start + width] = part
+            low[:, start : start + width] = part.astype(jnp.bfloat16)
+
+        def turn(_, carry):
+            gram = lax.dot_general(low[...], low[...], NT, preferred_element_type=jnp.float32)
+            gram_low = gram.astype(jnp.bfloat16)
+            twice = jnp.dot(gram_low, gram_low, preferred_element_type=jnp.float32)
+            blend[...] = (NS_B * gram + NS_C * twice).astype(jnp.bfloat16)
+
+            def piece(index, inner):
+                where = pl.ds(pl.multiple_of(index * width, width), width)
+                part = NS_A * wide[:, where] + jnp.dot(
+                    blend[...], low[:, where], preferred_element_type=jnp.float32
+                )
+                wide[:, where] = part
+                low[:, where] = part.astype(jnp.bfloat16)
+                return inner
+
+            return lax.fori_loop(0, total // width, piece, carry)
+
+        lax.fori_loop(0, 5, turn, 0)
+        if not turned:
+            for start in range(0, total, width):
+                held[start : start + width, :] = low[:, start : start + width].T
+
+    result = low if turned else held
+
+    def give(job, target, place):
+        @pl.when(me != target)
+        def _():
+            pltpu.make_async_remote_copy(
+                src_ref=slot(result, place), dst_ref=back.at[job],
+                send_sem=return_sem.at[target], recv_sem=back_sem.at[job],
+                device_id={"dp": target}, device_id_type=MESH,
+            ).start()
+
+        @pl.when(me == target)
+        def _():
+            back[job] = slot(result, place)[...]
+
+    def gave(target):
+        @pl.when(me != target)
+        def _():
+            pltpu.make_async_remote_copy(
+                src_ref=slot(result, 0), dst_ref=back.at[0],
+                send_sem=return_sem.at[target], recv_sem=back_sem.at[0],
+                device_id={"dp": target}, device_id_type=MESH,
+            ).wait_send()
+
+    jobs = (
+        (own_up, 0, 0, n_dp),
+        (own_down, 1, 0, n_dp),
+        (own_query, 2, 0, query_devices),
+        (own_out, 2, query_devices, n_dp),
+    )
+    for who, job, first, last in jobs:
+        @pl.when(me == who)
+        def _():
+            for target in range(first, last):
+                give(job, target, target - first)
+    rates = (LR_EXPERT, LR_EXPERT, jnp.where(me < query_devices, LR_QKV, LR_OUT))
+    for job in (2, 0, 1):
+        @pl.when(me != owners[job])
+        def _():
+            pltpu.make_async_remote_copy(
+                src_ref=outgoing.at[job], dst_ref=back.at[job],
+                send_sem=send_sem.at[job], recv_sem=back_sem.at[job],
+                device_id={"dp": owners[job]}, device_id_type=MESH,
+            ).wait()
+
+        step = rates[job] * turn_over(back[job]).astype(jnp.float32)
+        if job == 2:
+            new = dense_master[...] - step
+            dense_new[...] = new
+            dense_copy[...] = new.astype(jnp.bfloat16)
+        else:
+            new = expert_master[0, job] - step
+            expert_new[0, job] = new
+            expert_copy[0, job] = new.astype(jnp.bfloat16)
+    for who, job, first, last in jobs:
+        @pl.when(me == who)
+        def _():
+            for target in range(first, last):
+                gave(target)
+
+
+def muon(expert_grad, dense_grad, expert_momentum, dense_momentum, expert_master, dense_master):
+    n_dp = lax.axis_size("dp")
+    rows, width = dense_grad.shape
+    total = n_dp * rows
+    block = (width, rows) if rows % 128 == 0 else (rows, width)
+    whole = (width, total) if rows % 128 == 0 else (total, width)
+    full = jax.ShapeDtypeStruct(expert_grad.shape, jnp.float32)
+    flat = jax.ShapeDtypeStruct(dense_grad.shape, jnp.float32)
+    vmem = pl.BlockSpec(memory_space=pltpu.VMEM)
+    return pl.pallas_call(
+        partial(muon_kernel, n_dp, width),
+        out_shape=(
+            full, flat, full, flat,
+            jax.ShapeDtypeStruct(expert_grad.shape, jnp.bfloat16),
+            jax.ShapeDtypeStruct(dense_grad.shape, jnp.bfloat16),
+        ),
+        in_specs=[vmem] * 6,
+        out_specs=[vmem] * 6,
+        scratch_shapes=[
+            pltpu.VMEM((3, *block), jnp.bfloat16),
+            pltpu.VMEM(whole, jnp.bfloat16),
+            pltpu.VMEM((width, total), jnp.float32),
+            pltpu.VMEM((width, total), jnp.bfloat16),
+            pltpu.VMEM((width, width), jnp.bfloat16),
+            pltpu.VMEM((3, *block), jnp.bfloat16),
+            pltpu.SemaphoreType.DMA((3,)),
+            pltpu.SemaphoreType.DMA((n_dp,)),
+            pltpu.SemaphoreType.DMA((n_dp,)),
+            pltpu.SemaphoreType.DMA((3,)),
+        ],
+        compiler_params=pltpu.CompilerParams(
+            collective_id=1, has_side_effects=True, vmem_limit_bytes=48 * 1024 * 1024
+        ),
+        name="muon",
+    )(expert_grad, dense_grad, expert_momentum, dense_momentum, expert_master, dense_master)
 
 
 def shards(
@@ -290,69 +506,11 @@
         lax.psum(summed_dense.astype(jnp.bfloat16), "expert").astype(jnp.float32),
         lax.psum(summed_norm.astype(jnp.bfloat16), "expert").astype(jnp.float32),
     )
-    dense_moment = DECAY * dense_momentum + dense_grad
     norm_moment = DECAY * norm_momentum + norm_grad
-    expert_moment = DECAY * expert_momentum + expert_grad
-    row_start = lax.axis_index("dp")
-    dense_rows = dense_master.shape[0]
-    hidden_rows = expert_master.shape[2]
-    slot_ids = jnp.arange(dp_count)
-    dense_owner = jnp.where(row_start * dense_rows >= 3 * width, 3, 2)
-    dense_send = jnp.where((slot_ids == dense_owner)[:, None, None], dense_moment[None], 0.0)
-    expert_pick = slot_ids[:, None] == jnp.arange(2)[None, :]
-    expert_send = jnp.where(expert_pick[:, :, None, None], expert_moment[0][None], 0.0)
-    dense_got, expert_got = (
-        lax.all_to_all(
-            dense_send.astype(jnp.bfloat16), "dp", split_axis=0, concat_axis=0, tiled=True
-        ).astype(dense_send.dtype),
-        lax.all_to_all(
-            expert_send.astype(jnp.bfloat16), "dp", split_axis=0, concat_axis=0, tiled=True
-        ).astype(expert_send.dtype),
-    )
-    dense_gathered = dense_got.reshape(dp_count * dense_rows, width)
-    expert_gathered = expert_got.transpose(1, 0, 2, 3).reshape(2, dp_count * hidden_rows, width)
-    dense_zero = jnp.zeros((dp_count * dense_rows, width), jnp.float32)
-    expert_zero = jnp.zeros((2, dp_count * hidden_rows, width), jnp.float32)
-
-    def own_upper():
-        return (dense_zero, expert_zero.at[0].set(orthogonalize(expert_gathered[0])))
-
-    def own_lower():
-        return (dense_zero, expert_zero.at[1].set(orthogonalize(expert_gathered[1])))
-
-    def own_query():
-        return (
-            dense_zero.at[: 3 * width].set(LR_QKV * orthogonalize(dense_gathered[: 3 * width])),
-            expert_zero,
-        )
-
-    def own_output():
-        return (
-            dense_zero.at[3 * width :].set(LR_OUT * orthogonalize(dense_gathered[3 * width :])),
-            expert_zero,
-        )
-
-    def own_nothing():
-        return (dense_zero, expert_zero)
-
-    dense_dir, expert_dir = lax.switch(
-        jnp.minimum(row_start, 4), [own_upper, own_lower, own_query, own_output, own_nothing]
-    )
-    dense_back = dense_dir.reshape(dp_count, dense_rows, width)
-    expert_back = expert_dir.reshape(2, dp_count, hidden_rows, width).transpose(1, 0, 2, 3)
-    dense_ret, expert_ret = (
-        lax.all_to_all(
-            for_sending(dense_back), "dp", split_axis=0, concat_axis=0, tiled=True
-        ).astype(dense_back.dtype),
-        lax.all_to_all(
-            for_sending(expert_back), "dp", split_axis=0, concat_axis=0, tiled=True
-        ).astype(expert_back.dtype),
-    )
-    dense_step = jnp.sum(dense_ret, axis=0)
-    expert_shard = jnp.sum(expert_ret, axis=0)[None]
-    dense_new = dense_master - dense_step
     norm_new = norm_master - LR_VECTOR * tokens_all ** (-0.5) * norm_moment
-    expert_new = expert_master - LR_EXPERT * expert_shard
+    expert_moment, dense_moment, expert_new, dense_new, expert_copy, dense_copy = muon(
+        expert_grad, dense_grad, expert_momentum, dense_momentum, expert_master, dense_master
+    )
     return (
         jnp.stack(outputs_list),
         jnp.stack(input_list),
@@ -365,8 +523,8 @@
         dense_new,
         norm_new,
         expert_new,
-        dense_new.astype(jnp.bfloat16),
-        expert_new.astype(jnp.bfloat16),
+        dense_copy,
+        expert_copy,
     )
 
 

time: 710 us -> 502 us (0.71)
  starting transfers between devices: 144 us -> 35.3 us
  waiting for transfers between devices: 246 us -> 170 us
  Pallas kernels: 0 us -> 50.5 us
  loops' own time: 40.2 us -> 0 us
  other arithmetic: 65.9 us -> 47.3 us
  local copies, waits for them, and re-layouts: 66.2 us -> 54.6 us
    all_to_all x4 -> x0, starting transfers between devices: 109 us -> none  [the longest x1 89 us: shards(): lax.all_to_all(for_sending(dense_back), 'dp', split_axis=0, concat_axis=0...]
    pallas_call x0 -> x1, Pallas kernels: none -> 50.5 us  [muon(): pl.pallas_call(partial(muon_kernel, n_dp, width), out_shape=(full, flat,...]
    all_to_all x4 -> x0, waiting for transfers between devices: 44.7 us -> none  [the longest x1 39.7 us: shards(): lax.all_to_all(expert_send.astype(jnp.bfloat16), 'dp', split_axis=0, conc...]
    another operation x1 -> x0, loops' own time: 40.2 us -> none  [shards(): lax.switch(jnp.minimum(row_start, 4), [own_upper, own_lower, own_query, o...]
    all_to_all x2, waiting for transfers between devices: 0.01 us -> 36.5 us  [shards(): lax.all_to_all(produced.reshape(sources, count, features), 'expert', spli...]
    unnamed x7, waiting for transfers between devices: 33.7 us -> 0.1 us
    psum x1, waiting for transfers between devices: 26.1 us -> 0.01 us  [shards(): lax.psum(summed_dense.astype(jnp.bfloat16), 'expert').astype(jnp.float32)]
    reduce_scatter x1, waiting for transfers between devices: 26.2 us -> 16.1 us  [shards(): lax.psum_scatter(grad_dense.astype(jnp.bfloat16), 'dp', scatter_dimension...]
  transfers between devices with their start and end apart: 18 -> 14, of which waited for: 10 -> 8; matrix products, arithmetic and copies ran while one was open for 24% -> 28% of each run, Pallas kernels for 0% -> 0%
where the time goes in v1:
time: 502 us; the launch traced here: 496 us
  waiting for transfers between devices  170 us (34%)
  matrix products  105 us (21%)
  local copies, waits for them, and re-layouts  54.6 us (11%)
  Pallas kernels  50.5 us (10%)
  other arithmetic  47.3 us (9%)
  starting transfers between devices  35.3 us (7%)
  blocking collectives  17 us (3%)
  between operations  16 us (3%)
    reduce_scatter x1, waiting for transfers between devices, shards(): lax.psum_scatter(expert_terms.astype(jnp.bfloat16), 'dp', scatter_dimensi...  53.6 us
    pallas_call x1, Pallas kernels, muon(): pl.pallas_call(partial(muon_kernel, n_dp, width), out_shape=(full, flat,...  50.5 us
    all_to_all x2, waiting for transfers between devices, shards(): lax.all_to_all(produced.reshape(sources, count, features), 'expert', spli...  36.5 us
    dot_general x2, matrix products, shards(): jnp.einsum('rd,fd->rf', rows_in, w_up, preferred_element_type=jnp.float32)  35.3 us
    all_to_all x2, waiting for transfers between devices, shards(): lax.all_to_all(send.reshape(experts, capacity, width), 'expert', split_ax...  32.1 us
    all_to_all x2, waiting for transfers between devices, shards(): lax.all_to_all(grad_send.reshape(experts, capacity, width), 'expert', spl...  16.8 us
    reduce_scatter x1, waiting for transfers between devices, shards(): lax.psum_scatter(grad_dense.astype(jnp.bfloat16), 'dp', scatter_dimension...  16.1 us
    unnamed x212, local copies, waits for them, and re-layouts  15.2 us
  transfers between devices with their start and end apart: 14, of which 8 were waited for; matrix products, arithmetic and copies ran while one was open for 28% of the time, Pallas kernels for 0%

profile of v1, /device:TPU:5, one launch (start us, length us, event | category | flops | bytes accessed | tf_op | source)
XLA Modules:
  0.0 495.5 jit_solution(10180383335464667398)
XLA Ops:
  12.7 7.3 %select_reduce_fusion.1 = f32[788,197]{0,1:T(8,128)S(1)} fusion(f32[197,2]{1,0:T(8,128)S(1)} %copy.167, s32[197,2]{1,0:T(8,128)S(1)} %copy.155), kind=kLoop, calls=%fused_computation.66 | loop fusion | flops 776180 | bytes 624096 | tf_op jit(solution)/shard_map/reduce_sum | solution.py:432
  22.1 4.6 all-to-all-start.4
  27.6 9.9 %all-gather = bf16[8,64,4]{1,2,0:T(4,128)(2,1)S(1)} all-gather(bf16[1,64,4]{1,2,0:T(4,128)(2,1)S(1)} %convert_bitcast_fusion.2), channel_id=1, replica_groups=mesh['dp'=8,'expert'=4] {'dp'}, dimensions={0}, use_global_device_ids=true | all-gather | bytes 4608 | tf_op jit(solution)/shard_map/all_gather | solution.py:388
  40.6 7.4 %select_reduce_fusion = f32[788,197]{0,1:T(8,128)S(1)} fusion(f32[197,2]{1,0:T(8,128)S(1)} %copy.175, s32[197,2]{1,0:T(8,128)S(1)} %copy.162), kind=kLoop, calls=%fused_computation.65 | loop fusion | flops 776180 | bytes 624096 | tf_op jit(solution)/shard_map/reduce_sum | solution.py:432
  69.1 5.4 %all-to-all-start.6 = ((bf16[4,197,512]{2,1,0:T(8,128)(2,1)}), bf16[4,197,512]{2,1,0:T(8,128)(2,1)}, u32[]{:S(2)}, u32[]{:S(2)}) async-start(bf16[4,197,512]{2,1,0:T(8,128)(2,1)} %reshape.1147), calls=%async_computation.6 | async-start | bytes 1638400 | tf_op jit(solution)/shard_map/all_to_all | solution.py:434
  78.2 16.8 %all-to-all-done.6 = bf16[4,197,512]{2,1,0:T(8,128)(2,1)} async-done(((bf16[4,197,512]{2,1,0:T(8,128)(2,1)}), bf16[4,197,512]{2,1,0:T(8,128)(2,1)}, u32[]{:S(2)}, u32[]{:S(2)}) %all-to-all-start.6) | async-done | bytes 806944 | tf_op jit(solution)/shard_map/all_to_all | solution.py:434
  104.4 15.3 %all-to-all-done = bf16[4,197,512]{2,1,0:T(8,128)(2,1)} async-done(((bf16[4,197,512]{2,1,0:T(8,128)(2,1)}), bf16[4,197,512]{2,1,0:T(8,128)(2,1)}, u32[]{:S(2)}, u32[]{:S(2)}) %all-to-all-start) | async-done | bytes 806944 | tf_op jit(solution)/shard_map/all_to_all | solution.py:407
  126.8 16.7 %all-to-all-done.2 = bf16[4,197,512]{2,1,0:T(8,128)(2,1)S(1)} async-done(((bf16[4,197,512]{2,1,0:T(8,128)(2,1)}), bf16[4,197,512]{2,1,0:T(8,128)(2,1)S(1)}, u32[]{:S(2)}, u32[]{:S(2)}) %all-to-all-start.2) | async-done | bytes 806944 | tf_op jit(solution)/shard_map/all_to_all | solution.py:407
  144.6 17.8 %multiply_convert_fusion = (bf16[788,2048]{1,0:T(8,128)(2,1)}, f32[788,2048]{1,0:T(8,128)S(1)}, f32[788,2048]{1,0:T(8,128)S(1)}) fusion(bf16[788,512]{1,0:T(8,128)(2,1)} %reshape.1139, bf16[1,2,2048,512]{3,2,1,0:T(8,128)(2,1)} %all-gather.6.cloned.1.call-done), kind=kOutput, calls=%fused_computation.10 | convolution fusion | flops 1757454336 | bytes 19046400 | tf_op jit(solution)/shard_map/rd,fd->rf/dot_general | solution.py:416
  174.7 17.5 %multiply_convert_fusion.1 = (bf16[788,2048]{1,0:T(8,128)(2,1)}, f32[788,2048]{1,0:T(8,128)S(1)}, f32[788,2048]{1,0:T(8,128)S(1)}) fusion(bf16[788,512]{1,0:T(8,128)(2,1)S(1)} %reshape.1129, bf16[1,2,2048,512]{3,2,1,0:T(8,128)(2,1)} %all-gather.6.cloned.1.call-done), kind=kOutput, calls=%fused_computation.23 | convolution fusion | flops 1757454336 | bytes 19042304 | tf_op jit(solution)/shard_map/rd,fd->rf/dot_general | solution.py:416
  200.5 4.5 all-to-all-start.5
  210.8 14.6 %all-to-all-done.5 = bf16[4,197,512]{2,1,0:T(8,128)(2,1)S(1)} async-done(((bf16[4,197,512]{2,1,0:T(8,128)(2,1)}), bf16[4,197,512]{2,1,0:T(8,128)(2,1)S(1)}, u32[]{:S(2)}, u32[]{:S(2)}) %all-to-all-start.5) | async-done | bytes 806944 | tf_op jit(solution)/shard_map/all_to_all | solution.py:457
  254.6 4.7 fusion.163
  259.3 4.5 fusion.164
  271.0 6.9 %fusion.14 = bf16[1,1,2048,512]{3,2,1,0:T(8,128)(2,1)} fusion(f32[2048,512]{1,0:T(8,128)} %fusion.164, bf16[788,2048]{1,0:T(8,128)(2,1)} %get-tuple-element.117, bf16[788,512]{1,0:T(8,128)(2,1)S(1)} %copy-done.43), kind=kOutput, calls=%fused_computation.44 | convolution fusion | flops 1654652928 | bytes 10326016 | tf_op jit(solution)/shard_map/rf,rd->fd/dot_general | solution.py:445
  277.9 16.1 %reduce-scatter.6.cloned.1.call-done = bf16[256,512]{1,0:T(8,128)(2,1)} async-done(((bf16[2048,512]{1,0:T(8,128)(2,1)}), bf16[256,512]{1,0:T(8,128)(2,1)}) %reduce-scatter.6.cloned.1.call-update) | async-done | bytes 262160 | tf_op jit(solution)/shard_map/reduce_scatter | solution.py:495
  294.1 4.6 pad_maximum_fusion
  304.3 4.5 all-to-all-start.3
  308.7 4.5 convolution_convert_fusion.6
  314.3 14.8 %all-to-all-done.3 = bf16[4,197,512]{2,1,0:T(8,128)(2,1)S(1)} async-done(((bf16[4,197,512]{2,1,0:T(8,128)(2,1)}), bf16[4,197,512]{2,1,0:T(8,128)(2,1)S(1)}, u32[]{:S(2)}, u32[]{:S(2)}) %all-to-all-start.3) | async-done | bytes 806944 | tf_op jit(solution)/shard_map/all_to_all | solution.py:419
  336.2 21.8 %all-to-all-done.1 = bf16[4,197,512]{2,1,0:T(8,128)(2,1)} async-done(((bf16[4,197,512]{2,1,0:T(8,128)(2,1)}), bf16[4,197,512]{2,1,0:T(8,128)(2,1)}, u32[]{:S(2)}, u32[]{:S(2)}) %all-to-all-start.1) | async-done | bytes 806944 | tf_op jit(solution)/shard_map/all_to_all | solution.py:419
  368.4 7.1 %psum.15 = bf16[4,64]{1,0:T(4,128)(2,1)S(1)} all-reduce(bf16[4,64]{1,0:T(4,128)(2,1)S(1)} %copy.193), channel_id=1, replica_groups=mesh['dp'=8,'expert'=4] {'expert'}, use_global_device_ids=true, to_apply=%region_37.38 | all-reduce | flops 256 | bytes 1024 | tf_op jit(solution)/shard_map/psum | solution.py:507
  377.2 53.6 %reduce-scatter.8.cloned.1.call-done = bf16[1,2,256,512]{3,2,1,0:T(8,128)(2,1)} async-done(((bf16[1,2,2048,512]{3,2,1,0:T(8,128)(2,1)}), bf16[1,2,256,512]{3,2,1,0:T(8,128)(2,1)}) %reduce-scatter.8.cloned.1.call-update) | async-done | bytes 524304 | tf_op jit(solution)/shard_map/reduce_scatter | solution.py:501
  432.9 50.5 %muon.1 = (f32[1,2,256,512]{3,2,1,0:T(8,128)S(1)}, f32[256,512]{1,0:T(8,128)S(1)}, f32[1,2,256,512]{3,2,1,0:T(8,128)S(1)}, f32[256,512]{1,0:T(8,128)S(1)}, bf16[...) custom-call(f32[1,2,256,512]{3,2,1,0:T(8,128)} %convert_element_type.389.expert_grad, ...), custom_call_target="tpu_custom_call" | custom-call | tf_op jit(solution)/shard_map/muon/pallas_call | solution.py:326
  (369 shorter events, 148.1 us)
Async XLA Ops:
  7.2 50.4 %all-gather.4.cloned.1.call-start = ((), (), s32[]{:S(2)}) async-start(), calls=%async_computation.11 | async-start | bytes 2359296 | tf_op jit(solution)/shard_map/all_gather | solution.py:387
  12.7 35.4 %copy-start.31 = (bf16[1,1,197,512]{3,0,2,1:T(2,128)(2,1)}, bf16[1,1,197,512]{3,0,2,1:T(2,128)(2,1)S(1)}, u32[]{:S(2)}) copy-start(bf16[1,1,197,512]{3,0,2,1:T(2,128)(2,1)S(1)} %get-tuple-element.132) | copy-start | bytes 605188
  22.1 47.0 %all-to-all-start.4 = ((bf16[4,197,512]{2,1,0:T(8,128)(2,1)}), bf16[4,197,512]{2,1,0:T(8,128)(2,1)S(1)}, u32[]{:S(2)}, u32[]{:S(2)}) async-start(bf16[4,197,512]{2,1,0:T(8,128)(2,1)} %reshape.1142), calls=%async_computation.4 | async-start | bytes 1638400 | tf_op jit(solution)/shard_map/all_to_all | solution.py:434
  26.7 117.9 %all-gather.6.cloned.1.call-start = ((), (), s32[]{:S(2)}) async-start(), calls=%async_computation.12 | async-start | bytes 4718592 | tf_op jit(solution)/shard_map/all_gather | solution.py:374
  51.5 48.3 %copy-start.11 = (bf16[1,1,197,512]{3,2,1,0:T(8,128)(2,1)}, bf16[1,1,197,512]{3,2,1,0:T(8,128)(2,1)S(1)}, u32[]{:S(2)}) copy-start(bf16[1,1,197,512]{3,2,1,0:T(8,128)(2,1)S(1)} %get-tuple-element.122) | copy-start | bytes 605188
  57.5 44.7 %copy-start.53 = (f32[1,512]{1,0:T(1,128)}, f32[1,512]{1,0:T(1,128)S(1)}, u32[]{:S(2)}) copy-start(f32[1,512]{1,0:T(1,128)S(1)} %get-tuple-element.139) | copy-start | bytes 6148
  59.9 39.3 %copy-start.22 = (bf16[197,1536]{0,1:T(8,128)(2,1)}, bf16[197,1536]{0,1:T(8,128)(2,1)S(1)}, u32[]{:S(2)}) copy-start(bf16[197,1536]{0,1:T(8,128)(2,1)S(1)} %copy.160) | copy-start | bytes 1815556
  69.1 26.0 %all-to-all-start.6 = ((bf16[4,197,512]{2,1,0:T(8,128)(2,1)}), bf16[4,197,512]{2,1,0:T(8,128)(2,1)}, u32[]{:S(2)}, u32[]{:S(2)}) async-start(bf16[4,197,512]{2,1,0:T(8,128)(2,1)} %reshape.1147), calls=%async_computation.6 | async-start | bytes 1638400 | tf_op jit(solution)/shard_map/all_to_all | solution.py:434
  95.0 24.6 %all-to-all-start = ((bf16[4,197,512]{2,1,0:T(8,128)(2,1)}), bf16[4,197,512]{2,1,0:T(8,128)(2,1)}, u32[]{:S(2)}, u32[]{:S(2)}) async-start(bf16[4,197,512]{2,1,0:T(8,128)(2,1)} %reshape.1128), calls=%async_computation | async-start | bytes 1638400 | tf_op jit(solution)/shard_map/all_to_all | solution.py:407
  119.7 23.8 %all-to-all-start.2 = ((bf16[4,197,512]{2,1,0:T(8,128)(2,1)}), bf16[4,197,512]{2,1,0:T(8,128)(2,1)S(1)}, u32[]{:S(2)}, u32[]{:S(2)}) async-start(bf16[4,197,512]{2,1,0:T(8,128)(2,1)} %reshape.1138), calls=%async_computation.2 | async-start | bytes 1638400 | tf_op jit(solution)/shard_map/all_to_all | solution.py:407
  123.4 68.8 %copy-start.44 = (bf16[788,512]{1,0:T(8,128)(2,1)}, bf16[788,512]{1,0:T(8,128)(2,1)S(1)}, u32[]{:S(2)}) copy-start(bf16[788,512]{1,0:T(8,128)(2,1)S(1)} %reshape.1143) | copy-start | bytes 2420740
  125.1 37.3 %copy-start.42 = (bf16[788,512]{1,0:T(8,128)(2,1)}, bf16[788,512]{1,0:T(8,128)(2,1)S(1)}, u32[]{:S(2)}) copy-start(bf16[788,512]{1,0:T(8,128)(2,1)S(1)} %reshape.1148) | copy-start | bytes 2420740
  126.8 47.9 %copy-start.46 = (bf16[788,512]{1,0:T(8,128)(2,1)}, bf16[788,512]{1,0:T(8,128)(2,1)S(1)}, u32[]{:S(2)}) copy-start(bf16[788,512]{1,0:T(8,128)(2,1)S(1)} %reshape.1129) | copy-start | bytes 2420740
  170.7 29.8 %all-to-all-start.7 = ((bf16[4,197,512]{2,1,0:T(8,128)(2,1)}), bf16[4,197,512]{2,1,0:T(8,128)(2,1)S(1)}, u32[]{:S(2)}, u32[]{:S(2)}) async-start(bf16[4,197,512]{2,1,0:T(8,128)(2,1)} %reshape.1149), calls=%async_computation.7 | async-start | bytes 1638400 | tf_op jit(solution)/shard_map/all_to_all | solution.py:457
  200.5 24.9 %all-to-all-start.5 = ((bf16[4,197,512]{2,1,0:T(8,128)(2,1)}), bf16[4,197,512]{2,1,0:T(8,128)(2,1)S(1)}, u32[]{:S(2)}, u32[]{:S(2)}) async-start(bf16[4,197,512]{2,1,0:T(8,128)(2,1)} %reshape.1144), calls=%async_computation.5 | async-start | bytes 1638400 | tf_op jit(solution)/shard_map/all_to_all | solution.py:457
  205.0 89.1 %reduce-scatter.6.cloned.1.call-start = ((), (), s32[]{:S(2)}) async-start(), calls=%async_computation.13 | async-start | bytes 2359296 | tf_op jit(solution)/shard_map/reduce_scatter | solution.py:495
  254.1 113.5 %reduce-scatter.10.cloned.1.call-start = ((), (), s32[]{:S(2)}) async-start(), calls=%async_computation.16 | async-start | bytes 147456
  270.9 105.2 %all-reduce.2.cloned.1.call-start = ((), (), s32[]{:S(2)}) async-start(), calls=%async_computation.14 | async-start | bytes 524288 | tf_op jit(solution)/shard_map/psum | solution.py:506
  294.1 136.7 %reduce-scatter.8.cloned.1.call-start = ((), (), s32[]{:S(2)}) async-start(), calls=%async_computation.15 | async-start | bytes 4718592 | tf_op jit(solution)/shard_map/reduce_scatter | solution.py:501
  304.3 24.8 %all-to-all-start.3 = ((bf16[4,197,512]{2,1,0:T(8,128)(2,1)}), bf16[4,197,512]{2,1,0:T(8,128)(2,1)S(1)}, u32[]{:S(2)}, u32[]{:S(2)}) async-start(bf16[4,197,512]{2,1,0:T(8,128)(2,1)} %reshape.1140), calls=%async_computation.3 | async-start | bytes 1638400 | tf_op jit(solution)/shard_map/all_to_all | solution.py:419
  329.1 28.8 %all-to-all-start.1 = ((bf16[4,197,512]{2,1,0:T(8,128)(2,1)}), bf16[4,197,512]{2,1,0:T(8,128)(2,1)}, u32[]{:S(2)}, u32[]{:S(2)}) async-start(bf16[4,197,512]{2,1,0:T(8,128)(2,1)} %reshape.1130), calls=%async_computation.1 | async-start | bytes 1638400 | tf_op jit(solution)/shard_map/all_to_all | solution.py:419
  365.0 67.9 %copy-start = (f32[256,512]{1,0:T(8,128)S(1)}, f32[256,512]{1,0:T(8,128)}, u32[]{:S(2)}) copy-start(f32[256,512]{1,0:T(8,128)} %dense_master.1) | copy-start | bytes 1572868
  365.0 67.9 %copy-start.2 = (f32[256,512]{1,0:T(8,128)S(1)}, f32[256,512]{1,0:T(8,128)}, u32[]{:S(2)}) copy-start(f32[256,512]{1,0:T(8,128)} %dense_momentum.1) | copy-start | bytes 1572868
  377.1 108.1 %copy-start.1 = (f32[256,512]{1,0:T(8,128)}, f32[256,512]{1,0:T(8,128)S(1)}, u32[]{:S(2)}) copy-start(f32[256,512]{1,0:T(8,128)S(1)} %convert_element_type.386.dense_grad) | copy-start | bytes 1572868
  (91 other events, 606.3 us)
Sparse Core Ops, SparseCore 0:
  10.4 29.3 all-gather.3
  42.3 36.4 all-gather.5
  254.2 39.7 reduce-scatter.5
  297.5 33.3 reduce-scatter.9
  333.1 41.6 all-reduce.1
  378.0 52.6 reduce-scatter.7

commit v2 on v1

--- a/solution.py
+++ b/solution.py
@@ -9,6 +9,14 @@
 
 MESH = pl.DeviceIdType.MESH
 NT = (((1,), (1,)), ((), ()))
+TN = (((0,), (0,)), ((), ()))
+ERF_P = 0.3275911 * 0.5**0.5
+ERF_1 = 0.254829592
+ERF_2 = -0.284496736
+ERF_3 = 1.421413741
+ERF_4 = -1.453152027
+ERF_5 = 1.061405429
+ROOT_TWO_PI = 0.3989422804014327
 
 HEADS = 8
 
@@ -351,6 +359,675 @@
     )(expert_grad, dense_grad, expert_momentum, dense_momentum, expert_master, dense_master)
 
 
+def nn(a, b):
+    return jnp.dot(a, b, preferred_element_type=jnp.float32)
+
+
+def nt(a, b):
+    return lax.dot_general(a, b, NT, preferred_element_type=jnp.float32)
+
+
+def tn(a, b):
+    return lax.dot_general(a, b, TN, preferred_element_type=jnp.float32)
+
+
+def gelu_parts(pre):
+    bell = jnp.exp(-0.5 * pre * pre)
+    share = 1.0 / (1.0 + ERF_P * jnp.abs(pre))
+    series = share * (ERF_1 + share * (ERF_2 + share * (ERF_3 + share * (ERF_4 + share * ERF_5))))
+    tail = 0.5 * series * bell
+    return jnp.where(pre >= 0.0, 1.0 - tail, tail), bell * ROOT_TWO_PI
+
+
+def row_stats(rows):
+    mean = jnp.mean(rows, axis=-1, keepdims=True)
+    centred = rows - mean
+    inverse = lax.rsqrt(jnp.mean(centred * centred, axis=-1, keepdims=True) + NORM_EPS)
+    return centred * inverse, inverse
+
+
+def rows_backward(grad_out, normed, inverse, gain):
+    scaled = grad_out * gain
+    return inverse * (
+        scaled
+        - jnp.mean(scaled, axis=-1, keepdims=True)
+        - normed * jnp.mean(scaled * normed, axis=-1, keepdims=True)
+    )
+
+
+def block_kernel(
+    cfg, images, cotangent, weights, dense_master, norm_master, expert_master,
+    activations, input_grad, dense_grad, norm_grad, expert_grad,
+    dense, experts, norm_slots, norms, tokens, outer_low, normed_low, projected, soft, mixed, residual,
+    rows_x, rows_dy, turned_x, turned_dy, weight_slots, hidden_low, grad_pre_low,
+    produced_sum, grad_in_sum, produced_out, grad_in_out, produced_got, grad_in_got,
+    expert_sum, pair_out, pair_got, chip_got, grad_projected, grad_branch,
+    dense_sum, dense_out, dense_got, dense_chip, line_out, line_got, line_all, norm_all, norm_line,
+    dense_send, dense_take, expert_send, expert_take, norm_send, norm_take,
+    dy_send, dy_take, weight_send, weight_take, x_send, x_take, g_send, g_take, p_send, p_take,
+    pair_send, pair_take, chip_send, chip_take, dpair_send, dpair_take, dchip_send, dchip_take,
+    line_send, line_take, lall_send, lall_take, nall_send, nall_take, nline_send, nline_take,
+):
+    n_dp, n_ex, micro_count, seq, pad, width, heads = cfg
+    me, spot = lax.axis_index("dp"), lax.axis_index("expert")
+    core = lax.rem(me, 2)
+    partner = me + 1 - 2 * core
+    chips = n_dp // 2
+    chip = me // 2
+    bf16 = jnp.bfloat16
+    shard = expert_master.shape[2]
+    dense_shard = dense_master.shape[0]
+    norm_shard = norm_master.shape[1]
+    line_rows = n_ex * pad
+    head_size = width // heads
+    score_scale = head_size ** (-0.5)
+
+    def copy(src, dst, send, take, device):
+        return pltpu.make_async_remote_copy(
+            src_ref=src, dst_ref=dst, send_sem=send, recv_sem=take,
+            device_id=device, device_id_type=MESH,
+        )
+
+    def over_dp(step):
+        return lax.rem(me + step, n_dp)
+
+    def over_ex(step):
+        return lax.rem(spot + step, n_ex)
+
+    def at_row(ref, index, size):
+        return ref.at[pl.ds(pl.multiple_of(index * size, size), size)]
+
+    barrier = pltpu.get_barrier_semaphore()
+    for step in range(1, n_dp):
+        pl.semaphore_signal(barrier, inc=1, device_id={"dp": over_dp(step)}, device_id_type=MESH)
+    for step in range(1, n_ex):
+        pl.semaphore_signal(barrier, inc=1, device_id={"expert": over_ex(step)}, device_id_type=MESH)
+
+    at_row(dense, me, dense_shard)[...] = dense_master[...].astype(bf16)
+    for job in range(2):
+        at_row(experts.at[job], me, shard)[...] = expert_master[0, job].astype(bf16)
+    norm_slots[me] = jnp.zeros(norm_slots.shape[1:], jnp.float32)
+    norm_slots[me, 0:4, 0:norm_shard] = norm_master[...].astype(bf16).astype(jnp.float32)
+    weight_slots[spot] = weights[...]
+    tail = seq // 16 * 16
+    for micro in range(micro_count):
+        tokens[micro, tail:] = jnp.zeros((pad - tail, width), bf16)
+        tokens[micro, 0:seq] = images[micro]
+        outer_low[micro, tail:] = jnp.zeros((pad - tail, width), bf16)
+        outer_low[micro, 0:seq] = cotangent[micro]
+        rows_dy[micro, pl.ds(pl.multiple_of(spot * pad, 16), pad)] = outer_low[micro]
+        rows_x[micro, line_rows:] = jnp.zeros((rows_x.shape[1] - line_rows, width), bf16)
+        rows_dy[micro, line_rows:] = jnp.zeros((rows_x.shape[1] - line_rows, width), bf16)
+    hidden_low[line_rows:] = jnp.zeros((rows_x.shape[1] - line_rows, shard), bf16)
+    grad_pre_low[line_rows:] = jnp.zeros((rows_x.shape[1] - line_rows, shard), bf16)
+    pl.semaphore_wait(barrier, n_dp + n_ex - 2)
+
+    def gather_copy(views, source, target, send, take):
+        return [copy(view(source), view(source), send.at[k], take.at[k], {"dp": target}) for k, view in enumerate(views)]
+
+    def gather_start(views, send, take):
+        for step in range(0, n_dp, 2):
+            target = over_dp(step) if step else partner
+            for k, view in enumerate(views):
+                copy(view(me), view(me), send.at[k, step], take.at[k, me], {"dp": target}).start()
+
+    def gather_pass(views, send, take):
+        for step in range(2, n_dp, 2):
+            source = lax.rem(me + n_dp - step, n_dp)
+            for k, view in enumerate(views):
+                copy(view(source), view(source), send.at[k, step], take.at[k, source], {"dp": partner}).wait_recv()
+                copy(view(source), view(source), send.at[k, step + 1], take.at[k, source], {"dp": partner}).start()
+
+    def gather_end(views, send, take):
+        for step in range(0, n_dp, 2):
+            source = lax.rem(partner + n_dp - step, n_dp)
+            for k, view in enumerate(views):
+                copy(view(source), view(source), send.at[k, step], take.at[k, source], {"dp": partner}).wait_recv()
+        for step in range(n_dp):
+            if step != 1:
+                for k, view in enumerate(views):
+                    copy(view(me), view(me), send.at[k, step], take.at[k, me], {"dp": partner}).wait_send()
+
+    dense_views = [lambda i: at_row(dense, i, dense_shard)]
+    expert_views = [lambda i, job=job: at_row(experts.at[job], i, shard) for job in range(2)]
+    for step in range(1, n_dp):
+        copy(norm_slots.at[me], norm_slots.at[me], norm_send.at[step], norm_take.at[me], {"dp": over_dp(step)}).start()
+    gather_start(dense_views, dense_send, dense_take)
+
+    def line(ref, micro, index):
+        return ref.at[micro, pl.ds(pl.multiple_of(index * pad, 16), pad)]
+
+    def spread(ref, micro, send, take):
+        for step in range(1, n_ex):
+            copy(line(ref, micro, spot), line(ref, micro, spot), send.at[micro, step], take.at[micro, spot], {"expert": over_ex(step)}).start()
+
+    def spread_end(ref, micro, send, take):
+        for step in range(1, n_ex):
+            source = over_ex(step)
+            copy(line(ref, micro, source), line(ref, micro, source), send.at[micro, step], take.at[micro, source], {"expert": source}).wait()
+
+    for step in range(1, n_ex):
+        copy(weight_slots.at[spot], weight_slots.at[spot], weight_send.at[step], weight_take.at[spot], {"expert": over_ex(step)}).start()
+    spread(rows_dy, 0, dy_send, dy_take)
+
+    for step in range(1, n_dp):
+        source = over_dp(step)
+        copy(norm_slots.at[source], norm_slots.at[source], norm_send.at[step], norm_take.at[source], {"dp": source}).wait()
+    lane = lax.broadcasted_iota(jnp.int32, (128, width), 0)
+    column = lax.broadcasted_iota(jnp.int32, (128, width), 1)
+    wide = jnp.zeros((8, width), jnp.float32)
+    for index in range(n_dp):
+        pick = ((column - norm_shard * index == lane) & (lane < norm_shard)).astype(jnp.float32).astype(bf16)
+        wide = wide + nn(norm_slots[index].astype(bf16), pick)
+    norms[...] = wide
+
+    gather_pass(dense_views, dense_send, dense_take)
+    gather_start(expert_views, expert_send, expert_take)
+    gather_end(dense_views, dense_send, dense_take)
+
+    half = lax.broadcasted_iota(jnp.int32, (pad, 128), 1) < head_size
+    low_masks = [half.astype(jnp.float32).astype(bf16), (1.0 - half.astype(jnp.float32)).astype(bf16)]
+    real_key = lax.broadcasted_iota(jnp.int32, (pad, pad), 1) < seq
+
+    def pair_of(micro, part, index):
+        first = part * width + index * 128
+        return projected[micro, :, first : first + 128]
+
+    def attend(micro, carry):
+        normed, _ = row_stats(tokens[micro].astype(jnp.float32))
+        low = (normed * norms[0:1] + norms[1:2]).astype(bf16)
+        normed_low[micro] = low
+        projected[micro] = nt(low, dense[0 : 3 * width]).astype(bf16)
+        for index in range(heads // 2):
+            query, key, value = (pair_of(micro, part, index) for part in range(3))
+            parts = []
+            for side in range(2):
+                scores = nt(query * low_masks[side], key) * score_scale
+                scores = jnp.where(real_key, scores, -1e30)
+                top = jnp.max(scores, axis=-1, keepdims=True)
+                expo = jnp.exp(scores - top)
+                weight = expo / jnp.sum(expo, axis=-1, keepdims=True)
+                soft[micro, 2 * index + side] = weight
+                parts.append(nn(weight.astype(bf16), value))
+            mixed[micro, :, index * 128 : (index + 1) * 128] = jnp.where(half, parts[0], parts[1]).astype(bf16)
+        total = tokens[micro].astype(jnp.float32) + nt(mixed[micro], dense[3 * width :])
+        residual[micro] = total
+        normed, _ = row_stats(total)
+        line(rows_x, micro, spot)[...] = (normed * norms[2:3] + norms[3:4]).astype(bf16)
+        spread(rows_x, micro, x_send, x_take)
+        return carry
+
+    lax.fori_loop(0, micro_count, attend, 0)
+    for micro in range(1, micro_count):
+        spread(rows_dy, micro, dy_send, dy_take)
+    for step in range(1, n_ex):
+        source = over_ex(step)
+        copy(weight_slots.at[source], weight_slots.at[source], weight_send.at[step], weight_take.at[source], {"expert": source}).wait()
+    gather_pass(expert_views, expert_send, expert_take)
+    gather_end(expert_views, expert_send, expert_take)
+
+    def column_of(slot, micro, row):
+        picked = jnp.broadcast_to(weight_slots[slot, micro, pl.ds(row, 1)], (8, weight_slots.shape[3]))
+        return picked.T[0:pad, 0:1]
+
+    def send_back(out, got, micro, send, take):
+        for step in range(1, n_ex):
+            target = over_ex(step)
+            copy(line(out, micro, target), line(got, micro, spot), send.at[micro, step], take.at[micro, spot], {"expert": target}).start()
+
+    def send_back_end(out, got, micro, send, take):
+        for step in range(1, n_ex):
+            source = over_ex(step)
+            copy(line(out, micro, source), line(got, micro, source), send.at[micro, step], take.at[micro, source], {"expert": source}).wait()
+
+    for micro in range(micro_count):
+        spread_end(rows_dy, micro, dy_send, dy_take)
+        spread_end(rows_x, micro, x_send, x_take)
+        for block in range(n_ex):
+            where = slice(block * pad, (block + 1) * pad)
+            rows_dy[micro, where] = (column_of(block, micro, spot) * rows_dy[micro, where].astype(jnp.float32)).astype(bf16)
+        turned_x[...] = rows_x[micro].T
+        turned_dy[...] = rows_dy[micro].T
+        produced_sum[...] = jnp.zeros(produced_sum.shape, jnp.float32)
+        grad_in_sum[...] = jnp.zeros(grad_in_sum.shape, jnp.float32)
+        last = micro == micro_count - 1
+
+        def chunk(count, carry, micro=micro, last=last):
+            place = lax.rem(chip + 1 + count // 2, chips)
+            index = 2 * place + lax.rem(count, 2)
+            up = at_row(experts.at[0], index, shard)[...]
+            down = at_row(experts.at[1], index, shard)[...]
+            pre = nt(rows_x[micro, 0:line_rows], up)
+            below, density = gelu_parts(pre)
+            hidden_low[0:line_rows] = (pre * below).astype(bf16)
+            produced_sum[...] += nn(hidden_low[0:line_rows], down)
+            slope = below + pre * density
+            grad_pre_low[0:line_rows] = (nt(rows_dy[micro, 0:line_rows], down) * slope).astype(bf16)
+            grad_in_sum[...] += nn(grad_pre_low[0:line_rows], up)
+            up_grad = nn(turned_x[...], grad_pre_low[...])
+            down_grad = nn(turned_dy[...], hidden_low[...])
+            if micro > 0:
+                up_grad = up_grad + expert_sum[index, 0]
+                down_grad = down_grad + expert_sum[index, 1]
+            expert_sum[index, 0] = up_grad
+            expert_sum[index, 1] = down_grad
+            if last:
+                @pl.when(lax.rem(count, 2) != core)
+                def _():
+                    pair_out[place] = expert_sum[index].astype(bf16)
+                    copy(pair_out.at[place], pair_got.at[place], pair_send.at[place], pair_take.at[place], {"dp": partner}).start()
+
+                @pl.when((lax.rem(count, 2) == 1) & (count >= 3))
+                def _():
+                    chip_step(lax.rem(chip + count // 2, chips))
+            return carry
+
+        def chip_step(place):
+            index = 2 * place + core
+            copy(pair_out.at[place], pair_got.at[place], pair_send.at[place], pair_take.at[place], {"dp": partner}).wait()
+            for job in range(2):
+                pair_got[place, job] = (expert_sum[index, job] + pair_got[place, job].astype(jnp.float32)).astype(bf16)
+            copy(pair_got.at[place], chip_got.at[chip], chip_send.at[place], chip_take.at[chip], {"dp": index}).start()
+
+        lax.fori_loop(0, n_dp, chunk, 0)
+        grad_in_out[micro] = grad_in_sum[...].astype(bf16)
+        send_back(grad_in_out, grad_in_got, micro, g_send, g_take)
+        produced_out[micro] = produced_sum[...].astype(bf16)
+
+    def combine(out, got, micro):
+        line(got, micro, spot)[...] = line(out, micro, spot)[...]
+
+    def attend_back(micro, carry):
+        send_back_end(grad_in_out, grad_in_got, micro, g_send, g_take)
+        combine(grad_in_out, grad_in_got, micro)
+        incoming = jnp.zeros((pad, width), jnp.float32)
+        for index in range(n_ex):
+            incoming = incoming + grad_in_got[micro, index * pad : (index + 1) * pad].astype(jnp.float32)
+        normed, inverse = row_stats(residual[micro])
+        gain_two = jnp.sum(incoming * normed, axis=0, keepdims=True)
+        bias_two = jnp.sum(incoming, axis=0, keepdims=True)
+        total = outer_low[micro].astype(jnp.float32) + rows_backward(incoming, normed, inverse, norms[2:3])
+        branch_low = total.astype(bf16)
+        grad_branch[pl.ds(pl.multiple_of(micro * pad, 16), pad)] = branch_low
+        grad_mixed = nn(branch_low, dense[3 * width :]).astype(bf16)
+        for index in range(heads // 2):
+            query, key, value = (pair_of(micro, part, index) for part in range(3))
+            grad_pair = grad_mixed[:, index * 128 : (index + 1) * 128]
+            parts = []
+            for side in range(2):
+                weight = soft[micro, 2 * index + side]
+                grad_soft = nt(grad_pair * low_masks[side], value)
+                grad_scores = (
+                    weight * (grad_soft - jnp.sum(weight * grad_soft, axis=-1, keepdims=True))
+                ).astype(bf16)
+                parts.append((
+                    nn(grad_scores, key) * score_scale,
+                    tn(grad_scores, query) * score_scale,
+                    tn(weight.astype(bf16), grad_pair),
+                ))
+            for part in range(3):
+                first = part * width + index * 128
+                grad_projected[pl.ds(pl.multiple_of(micro * pad, 16), pad), first : first + 128] = jnp.where(
+                    half, parts[0][part], parts[1][part]
+                ).astype(bf16)
+        back = nn(grad_projected[pl.ds(pl.multiple_of(micro * pad, 16), pad)], dense[0 : 3 * width])
+        normed, inverse = row_stats(tokens[micro].astype(jnp.float32))
+        gain_one = jnp.sum(back * normed, axis=0, keepdims=True)
+        bias_one = jnp.sum(back, axis=0, keepdims=True)
+        total = total + rows_backward(back, normed, inverse, norms[0:1])
+        input_grad[micro] = total[0:seq].astype(bf16)
+        for row, part in enumerate((gain_one, bias_one, gain_two, bias_two)):
+            norm_all[me, row : row + 1] += part
+        return carry
+
+    norm_all[me] = jnp.zeros((8, width), jnp.float32)
+    depth = grad_branch.shape[0]
+    if depth > micro_count * pad:
+        grad_projected[micro_count * pad :] = jnp.zeros((depth - micro_count * pad, 3 * width), bf16)
+        grad_branch[micro_count * pad :] = jnp.zeros((depth - micro_count * pad, width), bf16)
+    lax.fori_loop(0, micro_count, attend_back, 0)
+
+    for micro in range(micro_count):
+        send_back(produced_out, produced_got, micro, p_send, p_take)
+    for step in range(1, n_dp):
+        copy(norm_all.at[me], norm_all.at[me], nall_send.at[step], nall_take.at[me], {"dp": over_dp(step)}).start()
+
+    depth = grad_branch.shape[0]
+    spare = [jnp.zeros((depth - micro_count * pad, width), bf16)] if depth > micro_count * pad else []
+    turned_x[:, 0:depth] = jnp.concatenate([normed_low[micro] for micro in range(micro_count)] + spare, axis=0).T
+    turned_dy[:, 0:depth] = jnp.concatenate([mixed[micro] for micro in range(micro_count)] + spare, axis=0).T
+
+    def dense_chunk(count, carry):
+        place = lax.rem(chip + 1 + count // 2, chips)
+        index = 2 * place + lax.rem(count, 2)
+        in_query = index * dense_shard < 3 * width
+
+        @pl.when(in_query)
+        def _():
+            dense_sum[chips] = nn(turned_x[:, 0:depth], grad_projected[:, pl.ds(pl.multiple_of(jnp.where(in_query, index, 0) * dense_shard, 128), dense_shard)])
+
+        @pl.when(jnp.logical_not(in_query))
+        def _():
+            first = jnp.where(in_query, 0, index * dense_shard - 3 * width)
+            dense_sum[chips] = nn(turned_dy[:, 0:depth], grad_branch[:, pl.ds(pl.multiple_of(first, 128), dense_shard)])
+
+        @pl.when(lax.rem(count, 2) == core)
+        def _():
+            dense_sum[place] = dense_sum[chips]
+
+        @pl.when(lax.rem(count, 2) != core)
+        def _():
+            dense_out[place] = dense_sum[chips].astype(bf16)
+            copy(dense_out.at[place], dense_got.at[place], dpair_send.at[place], dpair_take.at[place], {"dp": partner}).start()
+
+        @pl.when((lax.rem(count, 2) == 1) & (count >= 3))
+        def _():
+            before = lax.rem(chip + count // 2, chips)
+            copy(dense_out.at[before], dense_got.at[before], dpair_send.at[before], dpair_take.at[before], {"dp": partner}).wait()
+            dense_got[before] = (dense_sum[before] + dense_got[before].astype(jnp.float32)).astype(bf16)
+            copy(dense_got.at[before], dense_chip.at[chip], dchip_send.at[before], dchip_take.at[chip], {"dp": 2 * before + core}).start()
+        return carry
+
+    lax.fori_loop(0, n_dp, dense_chunk, 0)
+
+    copy(pair_out.at[chip], pair_got.at[chip], pair_send.at[chip], pair_take.at[chip], {"dp": partner}).wait()
+    for job in range(2):
+        expert_sum[me, job] = expert_sum[me, job] + pair_got[chip, job].astype(jnp.float32)
+    for step in range(1, chips):
+        place = lax.rem(chip + step, chips)
+        copy(pair_got.at[place], chip_got.at[place], chip_send.at[place], chip_take.at[place], {"dp": 2 * place + core}).wait()
+        for job in range(2):
+            expert_sum[me, job] = expert_sum[me, job] + chip_got[place, job].astype(jnp.float32)
+    for job in range(2):
+        expert_grad[0, job] = expert_sum[me, job].T
+
+    copy(dense_out.at[chip], dense_got.at[chip], dpair_send.at[chip], dpair_take.at[chip], {"dp": partner}).wait()
+    plane = dense_sum[chip] + dense_got[chip].astype(jnp.float32)
+    for step in range(1, chips):
+        place = lax.rem(chip + step, chips)
+        copy(dense_got.at[place], dense_chip.at[place], dchip_send.at[place], dchip_take.at[place], {"dp": 2 * place + core}).wait()
+        plane = plane + dense_chip[place].astype(jnp.float32)
+    quarter = width // n_ex
+    for index in range(n_ex):
+        line_out[index] = plane[index * quarter : (index + 1) * quarter].astype(bf16)
+    for step in range(1, n_ex):
+        target = over_ex(step)
+        copy(line_out.at[target], line_got.at[spot], line_send.at[step], line_take.at[spot], {"expert": target}).start()
+    for step in range(1, n_dp):
+        source = over_dp(step)
+        copy(norm_all.at[source], norm_all.at[source], nall_send.at[step], nall_take.at[source], {"dp": source}).wait()
+    norm_total = norm_all[0]
+    for index in range(1, n_dp):
+        norm_total = norm_total + norm_all[index]
+    norm_line[spot] = norm_total
+    for step in range(1, n_ex):
+        copy(norm_line.at[spot], norm_line.at[spot], nline_send.at[step], nline_take.at[spot], {"expert": over_ex(step)}).start()
+    summed = line_out[spot].astype(jnp.float32)
+    for step in range(1, n_ex):
+        source = over_ex(step)
+        copy(line_out.at[source], line_got.at[source], line_send.at[step], line_take.at[source], {"expert": source}).wait()
+        summed = summed + line_got[source].astype(jnp.float32)
+    line_all[spot] = summed.astype(bf16)
+    for step in range(1, n_ex):
+        copy(line_all.at[spot], line_all.at[spot], lall_send.at[step], lall_take.at[spot], {"expert": over_ex(step)}).start()
+
+    for micro in range(micro_count):
+        send_back_end(produced_out, produced_got, micro, p_send, p_take)
+        combine(produced_out, produced_got, micro)
+        total = residual[micro]
+        for index in range(n_ex):
+            gate = weight_slots[spot, micro].T[0:pad, index : index + 1]
+            total = total + gate * produced_got[micro, index * pad : (index + 1) * pad].astype(jnp.float32)
+        activations[micro] = total[0:seq].astype(bf16)
+
+    for step in range(1, n_ex):
+        source = over_ex(step)
+        copy(norm_line.at[source], norm_line.at[source], nline_send.at[step], nline_take.at[source], {"expert": source}).wait()
+        copy(line_all.at[source], line_all.at[source], lall_send.at[step], lall_take.at[source], {"expert": source}).wait()
+    norm_total = norm_line[0]
+    for index in range(1, n_ex):
+        norm_total = norm_total + norm_line[index]
+    for index in range(n_dp):
+        @pl.when(me == index)
+        def _():
+            norm_grad[...] = norm_total[0:4, index * norm_shard : (index + 1) * norm_shard]
+    for index in range(n_ex):
+        dense_grad[:, index * quarter : (index + 1) * quarter] = line_all[index].astype(jnp.float32).T
+
+
+def block(images, cotangent, gates, routes, dense_master, norm_master, expert_master):
+    micro_count, _, seq, width = images.shape
+    n_dp, n_ex = lax.axis_size("dp"), lax.axis_size("expert")
+    pad = -(-seq // 16) * 16
+    lanes = -(-seq // 128) * 128
+    shard, dense_shard, norm_shard = expert_master.shape[2], dense_master.shape[0], norm_master.shape[1]
+    chips = n_dp // 2
+    line_rows = n_ex * pad
+    line_pad = -(-line_rows // 128) * 128
+    slots = -(-n_ex // 8) * 8
+    depth = -(-micro_count * pad // 128) * 128
+    named = routes[:, 0, None, :, :] == jnp.arange(slots)[None, :, None, None]
+    weights = jnp.sum(jnp.where(named, gates[:, 0, None, :, :], 0.0), axis=3)
+    weights = jnp.pad(weights, ((0, 0), (0, 0), (0, lanes - seq)))
+    vmem = pl.BlockSpec(memory_space=pltpu.VMEM)
+    bf16, f32 = jnp.bfloat16, jnp.float32
+    dma = pltpu.SemaphoreType.DMA
+    tokens = (micro_count, pad, width)
+    scratch = [
+        pltpu.VMEM((n_dp * dense_shard, width), bf16),
+        pltpu.VMEM((2, n_dp * shard, width), bf16),
+        pltpu.VMEM((n_dp, 8, 128), f32),
+        pltpu.VMEM((8, width), f32),
+        pltpu.VMEM(tokens, bf16),
+        pltpu.VMEM(tokens, bf16),
+        pltpu.VMEM(tokens, bf16),
+        pltpu.VMEM((micro_count, pad, 3 * width), bf16),
+        pltpu.VMEM((micro_count, HEADS, pad, pad), f32),
+        pltpu.VMEM(tokens, bf16),
+        pltpu.VMEM(tokens, f32),
+        pltpu.VMEM((micro_count, line_pad, width), bf16),
+        pltpu.VMEM((micro_count, line_pad, width), bf16),
+        pltpu.VMEM((width, line_pad), bf16),
+        pltpu.VMEM((width, line_pad), bf16),
+        pltpu.VMEM((n_ex, micro_count, slots, lanes), f32),
+        pltpu.VMEM((line_pad, shard), bf16),
+        pltpu.VMEM((line_pad, shard), bf16),
+        pltpu.VMEM((line_rows, width), f32),
+        pltpu.VMEM((line_rows, width), f32),
+        pltpu.VMEM((micro_count, line_rows, width), bf16),
+        pltpu.VMEM((micro_count, line_rows, width), bf16),
+        pltpu.VMEM((micro_count, line_rows, width), bf16),
+        pltpu.VMEM((micro_count, line_rows, width), bf16),
+        pltpu.VMEM((n_dp, 2, width, shard), f32),
+        pltpu.VMEM((chips, 2, width, shard), bf16),
+        pltpu.VMEM((chips, 2, width, shard), bf16),
+        pltpu.VMEM((chips, 2, width, shard), bf16),
+        pltpu.VMEM((depth, 3 * width), bf16),
+        pltpu.VMEM((depth, width), bf16),
+        pltpu.VMEM((chips + 1, width, dense_shard), f32),
+        pltpu.VMEM((chips, width, dense_shard), bf16),
+        pltpu.VMEM((chips, width, dense_shard), bf16),
+        pltpu.VMEM((chips, width, dense_shard), bf16),
+        pltpu.VMEM((n_ex, width // n_ex, dense_shard), bf16),
+        pltpu.VMEM((n_ex, width // n_ex, dense_shard), bf16),
+        pltpu.VMEM((n_ex, width // n_ex, dense_shard), bf16),
+        pltpu.VMEM((n_dp, 8, width), f32),
+        pltpu.VMEM((n_ex, 8, width), f32),
+    ]
+    sems = [(1, n_dp), (1, n_dp), (2, n_dp), (2, n_dp), (n_dp,), (n_dp,)]
+    sems += [(micro_count, n_ex)] * 2 + [(n_ex,)] * 2 + [(micro_count, n_ex)] * 6
+    sems += [(chips,)] * 8 + [(n_ex,)] * 4 + [(n_dp,)] * 2 + [(n_ex,)] * 2
+    cfg = (n_dp, n_ex, micro_count, seq, pad, width, HEADS)
+    return pl.pallas_call(
+        partial(block_kernel, cfg),
+        out_shape=(
+            jax.ShapeDtypeStruct((micro_count, seq, width), bf16),
+            jax.ShapeDtypeStruct((micro_count, seq, width), bf16),
+            jax.ShapeDtypeStruct(dense_master.shape, f32),
+            jax.ShapeDtypeStruct(norm_master.shape, f32),
+            jax.ShapeDtypeStruct(expert_master.shape, f32),
+        ),
+        in_specs=[vmem] * 6,
+        out_specs=[vmem] * 5,
+        scratch_shapes=scratch + [dma(shape) for shape in sems],
+        compiler_params=pltpu.CompilerParams(
+            collective_id=2, has_side_effects=True, vmem_limit_bytes=67043328
+        ),
+        name="block",
+    )(images[:, 0], cotangent[:, 0], weights, dense_master, norm_master, expert_master)
+
+
+def block_plain(images, cotangent, gates, routes, slots, dense_master, norm_master, expert_master):
+    micro_count, images_here, seq, width = images.shape
+    experts = lax.axis_size("expert")
+    dp_count = lax.axis_size("dp")
+    rows_dev = images_here * seq
+    capacity = min(rows_dev, 4 * rows_dev // experts)
+    slot_total = experts * capacity
+    whole_experts = lax.all_gather(expert_master.astype(jnp.bfloat16), "dp", axis=2, tiled=True)
+    w_up = whole_experts[0, 0]
+    w_down = whole_experts[0, 1]
+    dense_low = dense_master.astype(jnp.bfloat16)
+    norm_low = norm_master.astype(jnp.bfloat16)
+    grad_dense = jnp.zeros((4 * width, width), jnp.float32)
+    grad_norm = jnp.zeros((4, width), jnp.float32)
+    grad_up = jnp.zeros(w_up.shape, jnp.float32)
+    grad_down = jnp.zeros(w_down.shape, jnp.float32)
+    outputs_list = []
+    input_list = []
+    for micro in range(micro_count):
+        dense_whole, norm_whole = (
+            lax.all_gather(dense_low, "dp", axis=0, tiled=True),
+            lax.all_gather(norm_low, "dp", axis=1, tiled=True),
+        )
+        norm_wide = norm_whole.astype(jnp.float32)
+        block = images[micro].astype(jnp.float32).reshape(rows_dev, width)
+        normed_full, normed_one, inverse_one = layer_norm(block, norm_wide[0], norm_wide[1])
+        normed_one_low = normed_full.astype(jnp.bfloat16).reshape(images_here, seq, width)
+        branch, kept = attention_forward(
+            normed_one_low, dense_whole[: 3 * width], dense_whole[3 * width :], HEADS
+        )
+        residual = block + branch.reshape(rows_dev, width)
+        normed_two_full, normed_two, inverse_two = layer_norm(residual, norm_wide[2], norm_wide[3])
+        normed_two_low = normed_two_full.astype(jnp.bfloat16)
+        index = (routes[micro] * capacity + slots[micro]).reshape(rows_dev, 2)
+        gate_pair = gates[micro].reshape(rows_dev, 2)
+        picks = jnp.arange(slot_total)[:, None, None] == index[None, :, :]
+        dispatch = jnp.sum(picks.astype(jnp.int32), axis=2).astype(jnp.bfloat16)
+        send = jnp.dot(dispatch, normed_two_low, preferred_element_type=jnp.float32).astype(
+            jnp.bfloat16
+        )
+        received = lax.all_to_all(
+            send.reshape(experts, capacity, width),
+            "expert",
+            split_axis=0,
+            concat_axis=0,
+            tiled=True,
+        )
+        sources, count, features = received.shape
+        rows_in = received.reshape(sources * count, features)
+        pre = jnp.einsum("rd,fd->rf", rows_in, w_up, preferred_element_type=jnp.float32)
+        hidden = jax.nn.gelu(pre, approximate=False).astype(jnp.bfloat16)
+        produced = jnp.dot(hidden, w_down, preferred_element_type=jnp.float32).astype(jnp.bfloat16)
+        returned = lax.all_to_all(
+            produced.reshape(sources, count, features),
+            "expert",
+            split_axis=0,
+            concat_axis=0,
+            tiled=True,
+        )
+        returned, received, pre = (returned, received, pre.reshape(sources, count, pre.shape[1]))
+        back_flat = returned.reshape(slot_total, width)
+        taken = back_flat[index].astype(jnp.float32)
+        moe = gate_pair[:, 0:1] * taken[:, 0] + gate_pair[:, 1:2] * taken[:, 1]
+        outputs_list.append((residual + moe).astype(jnp.bfloat16).reshape(images_here, seq, width))
+        grad_output = cotangent[micro].astype(jnp.float32).reshape(rows_dev, width)
+        spread = jnp.sum(jnp.where(picks, gate_pair[None, :, :], 0.0), axis=2)
+        grad_send = jnp.dot(spread, grad_output, precision=HIGH).astype(jnp.bfloat16)
+        grad_received = lax.all_to_all(
+            grad_send.reshape(experts, capacity, width),
+            "expert",
+            split_axis=0,
+            concat_axis=0,
+            tiled=True,
+        )
+        grad_rows_out = grad_received.reshape(slot_total, width)
+        pre_rows = pre.reshape(slot_total, pre.shape[2])
+        hidden_full, gelu_pull = jax.vjp(partial(jax.nn.gelu, approximate=False), pre_rows)
+        hidden = hidden_full.astype(jnp.bfloat16)
+        grad_down = grad_down + jnp.einsum(
+            "rf,rd->fd", hidden, grad_rows_out, preferred_element_type=jnp.float32
+        )
+        grad_hidden = jnp.einsum(
+            "rd,fd->rf", grad_rows_out, w_down, preferred_element_type=jnp.float32
+        )
+        grad_pre = gelu_pull(grad_hidden)[0].astype(jnp.bfloat16)
+        rows_in = received.reshape(slot_total, width)
+        grad_up = grad_up + jnp.einsum(
+            "rf,rd->fd", grad_pre, rows_in, preferred_element_type=jnp.float32
+        )
+        grad_in = jnp.dot(grad_pre, w_up, preferred_element_type=jnp.float32).astype(jnp.bfloat16)
+        grad_back = lax.all_to_all(
+            grad_in.reshape(experts, capacity, width),
+            "expert",
+            split_axis=0,
+            concat_axis=0,
+            tiled=True,
+        )
+        pair_back = grad_back.reshape(slot_total, width)[index].astype(jnp.float32)
+        grad_normed_two = pair_back[:, 0] + pair_back[:, 1]
+        grad_two_rows, gain_two_grad, bias_two_grad = norm_backward(
+            grad_normed_two, normed_two, inverse_two, norm_wide[2]
+        )
+        grad_residual = grad_output + grad_two_rows
+        dense_again, norm_again = (
+            lax.all_gather(dense_low, "dp", axis=0, tiled=True),
+            lax.all_gather(norm_low, "dp", axis=1, tiled=True),
+        )
+        norm_again_wide = norm_again.astype(jnp.float32)
+        grad_normed_one, grad_qkv_w, grad_out_w = attention_backward(
+            grad_residual.reshape(images_here, seq, width),
+            normed_one_low,
+            dense_again[: 3 * width],
+            dense_again[3 * width :],
+            kept,
+            HEADS,
+        )
+        grad_one_rows, gain_one_grad, bias_one_grad = norm_backward(
+            grad_normed_one.reshape(rows_dev, width), normed_one, inverse_one, norm_again_wide[0]
+        )
+        input_list.append(
+            (grad_residual + grad_one_rows).astype(jnp.bfloat16).reshape(images_here, seq, width)
+        )
+        grad_dense = grad_dense + jnp.concatenate([grad_qkv_w, grad_out_w], axis=0)
+        grad_norm = grad_norm + jnp.stack(
+            [gain_one_grad, bias_one_grad, gain_two_grad, bias_two_grad]
+        )
+    expert_terms = jnp.stack([grad_up, grad_down])[None]
+    summed_dense, summed_norm, expert_grad = (
+        lax.psum_scatter(
+            grad_dense.astype(jnp.bfloat16), "dp", scatter_dimension=0, tiled=True
+        ).astype(jnp.float32),
+        lax.psum_scatter(
+            grad_norm.astype(jnp.bfloat16), "dp", scatter_dimension=1, tiled=True
+        ).astype(jnp.float32),
+        lax.psum_scatter(
+            expert_terms.astype(jnp.bfloat16), "dp", scatter_dimension=2, tiled=True
+        ).astype(jnp.float32),
+    )
+    dense_grad, norm_grad = (
+        lax.psum(summed_dense.astype(jnp.bfloat16), "expert").astype(jnp.float32),
+        lax.psum(summed_norm.astype(jnp.bfloat16), "expert").astype(jnp.float32),
+    )
+    return (
+        jnp.stack(outputs_list),
+        jnp.stack(input_list),
+        dense_grad,
+        norm_grad,
+        expert_grad,
+    )
+
+
 def shards(
     images,
     cotangent,
@@ -367,153 +1044,25 @@
     micro_count, images_here, seq, width = images.shape
     experts = lax.axis_size("expert")
     dp_count = lax.axis_size("dp")
-    rows_dev = images_here * seq
-    capacity = min(rows_dev, 4 * rows_dev // experts)
-    slot_total = experts * capacity
-    tokens_all = micro_count * rows_dev * dp_count * experts
-    whole_experts = lax.all_gather(expert_master.astype(jnp.bfloat16), "dp", axis=2, tiled=True)
-    w_up = whole_experts[0, 0]
-    w_down = whole_experts[0, 1]
-    dense_low = dense_master.astype(jnp.bfloat16)
-    norm_low = norm_master.astype(jnp.bfloat16)
-    grad_dense = jnp.zeros((4 * width, width), jnp.float32)
-    grad_norm = jnp.zeros((4, width), jnp.float32)
-    grad_up = jnp.zeros(w_up.shape, jnp.float32)
-    grad_down = jnp.zeros(w_down.shape, jnp.float32)
-    outputs_list = []
-    input_list = []
-    for micro in range(micro_count):
-        dense_whole, norm_whole = (
-            lax.all_gather(dense_low, "dp", axis=0, tiled=True),
-            lax.all_gather(norm_low, "dp", axis=1, tiled=True),
-        )
-        norm_wide = norm_whole.astype(jnp.float32)
-        block = images[micro].astype(jnp.float32).reshape(rows_dev, width)
-        normed_full, normed_one, inverse_one = layer_norm(block, norm_wide[0], norm_wide[1])
-        normed_one_low = normed_full.astype(jnp.bfloat16).reshape(images_here, seq, width)
-        branch, kept = attention_forward(
-            normed_one_low, dense_whole[: 3 * width], dense_whole[3 * width :], HEADS
-        )
-        residual = block + branch.reshape(rows_dev, width)
-        normed_two_full, normed_two, inverse_two = layer_norm(residual, norm_wide[2], norm_wide[3])
-        normed_two_low = normed_two_full.astype(jnp.bfloat16)
-        index = (routes[micro] * capacity + slots[micro]).reshape(rows_dev, 2)
-        gate_pair = gates[micro].reshape(rows_dev, 2)
-        picks = jnp.arange(slot_total)[:, None, None] == index[None, :, :]
-        dispatch = jnp.sum(picks.astype(jnp.int32), axis=2).astype(jnp.bfloat16)
-        send = jnp.dot(dispatch, normed_two_low, preferred_element_type=jnp.float32).astype(
-            jnp.bfloat16
-        )
-        received = lax.all_to_all(
-            send.reshape(experts, capacity, width),
-            "expert",
-            split_axis=0,
-            concat_axis=0,
-            tiled=True,
-        )
-        sources, count, features = received.shape
-        rows_in = received.reshape(sources * count, features)
-        pre = jnp.einsum("rd,fd->rf", rows_in, w_up, preferred_element_type=jnp.float32)
-        hidden = jax.nn.gelu(pre, approximate=False).astype(jnp.bfloat16)
-        produced = jnp.dot(hidden, w_down, preferred_element_type=jnp.float32).astype(jnp.bfloat16)
-        returned = lax.all_to_all(
-            produced.reshape(sources, count, features),
-            "expert",
-            split_axis=0,
-            concat_axis=0,
-            tiled=True,
-        )
-        returned, received, pre = (returned, received, pre.reshape(sources, count, pre.shape[1]))
-        back_flat = returned.reshape(slot_total, width)
-        taken = back_flat[index].astype(jnp.float32)
-        moe = gate_pair[:, 0:1] * taken[:, 0] + gate_pair[:, 1:2] * taken[:, 1]
-        outputs_list.append((residual + moe).astype(jnp.bfloat16).reshape(images_here, seq, width))
-        grad_output = cotangent[micro].astype(jnp.float32).reshape(rows_dev, width)
-        spread = jnp.sum(jnp.where(picks, gate_pair[None, :, :], 0.0), axis=2)
-        grad_send = jnp.dot(spread, grad_output, precision=HIGH).astype(jnp.bfloat16)
-        grad_received = lax.all_to_all(
-            grad_send.reshape(experts, capacity, width),
-            "expert",
-            split_axis=0,
-            concat_axis=0,
-            tiled=True,
-        )
-        grad_rows_out = grad_received.reshape(slot_total, width)
-        pre_rows = pre.reshape(slot_total, pre.shape[2])
-        hidden_full, gelu_pull = jax.vjp(partial(jax.nn.gelu, approximate=False), pre_rows)
-        hidden = hidden_full.astype(jnp.bfloat16)
-        grad_down = grad_down + jnp.einsum(
-            "rf,rd->fd", hidden, grad_rows_out, preferred_element_type=jnp.float32
-        )
-        grad_hidden = jnp.einsum(
-            "rd,fd->rf", grad_rows_out, w_down, preferred_element_type=jnp.float32
-        )
-        grad_pre = gelu_pull(grad_hidden)[0].astype(jnp.bfloat16)
-        rows_in = received.reshape(slot_total, width)
-        grad_up = grad_up + jnp.einsum(
-            "rf,rd->fd", grad_pre, rows_in, preferred_element_type=jnp.float32
-        )
-        grad_in = jnp.dot(grad_pre, w_up, preferred_element_type=jnp.float32).astype(jnp.bfloat16)
-        grad_back = lax.all_to_all(
-            grad_in.reshape(experts, capacity, width),
-            "expert",
-            split_axis=0,
-            concat_axis=0,
-            tiled=True,
-        )
-        pair_back = grad_back.reshape(slot_total, width)[index].astype(jnp.float32)
-        grad_normed_two = pair_back[:, 0] + pair_back[:, 1]
-        grad_two_rows, gain_two_grad, bias_two_grad = norm_backward(
-            grad_normed_two, normed_two, inverse_two, norm_wide[2]
-        )
-        grad_residual = grad_output + grad_two_rows
-        dense_again, norm_again = (
-            lax.all_gather(dense_low, "dp", axis=0, tiled=True),
-            lax.all_gather(norm_low, "dp", axis=1, tiled=True),
-        )
-        norm_again_wide = norm_again.astype(jnp.float32)
-        grad_normed_one, grad_qkv_w, grad_out_w = attention_backward(
-            grad_residual.reshape(images_here, seq, width),
-            normed_one_low,
-            dense_again[: 3 * width],
-            dense_again[3 * width :],
-            kept,
-            HEADS,
-        )
-        grad_one_rows, gain_one_grad, bias_one_grad = norm_backward(
-            grad_normed_one.reshape(rows_dev, width), normed_one, inverse_one, norm_again_wide[0]
-        )
-        input_list.append(
-            (grad_residual + grad_one_rows).astype(jnp.bfloat16).reshape(images_here, seq, width)
-        )
-        grad_dense = grad_dense + jnp.concatenate([grad_qkv_w, grad_out_w], axis=0)
-        grad_norm = grad_norm + jnp.stack(
-            [gain_one_grad, bias_one_grad, gain_two_grad, bias_two_grad]
-        )
-    expert_terms = jnp.stack([grad_up, grad_down])[None]
-    summed_dense, summed_norm, expert_grad = (
-        lax.psum_scatter(
-            grad_dense.astype(jnp.bfloat16), "dp", scatter_dimension=0, tiled=True
-        ).astype(jnp.float32),
-        lax.psum_scatter(
-            grad_norm.astype(jnp.bfloat16), "dp", scatter_dimension=1, tiled=True
-        ).astype(jnp.float32),
-        lax.psum_scatter(
-            expert_terms.astype(jnp.bfloat16), "dp", scatter_dimension=2, tiled=True
-        ).astype(jnp.float32),
-    )
-    dense_grad, norm_grad = (
-        lax.psum(summed_dense.astype(jnp.bfloat16), "expert").astype(jnp.float32),
-        lax.psum(summed_norm.astype(jnp.bfloat16), "expert").astype(jnp.float32),
-    )
+    tokens_all = micro_count * images_here * seq * dp_count * experts
+    lined = dense_master.shape[0] % 128 == 0 and expert_master.shape[2] % 128 == 0
+    if lined and images_here == 1 and dp_count % 2 == 0 and width == 64 * HEADS:
+        out, grad, dense_grad, norm_grad, expert_grad = block(
+            images, cotangent, gates, routes, dense_master, norm_master, expert_master
+        )
+        out, grad = out[:, None], grad[:, None]
+    else:
+        out, grad, dense_grad, norm_grad, expert_grad = block_plain(
+            images, cotangent, gates, routes, slots, dense_master, norm_master, expert_master
+        )
     norm_moment = DECAY * norm_momentum + norm_grad
     norm_new = norm_master - LR_VECTOR * tokens_all ** (-0.5) * norm_moment
     expert_moment, dense_moment, expert_new, dense_new, expert_copy, dense_copy = muon(
         expert_grad, dense_grad, expert_momentum, dense_momentum, expert_master, dense_master
     )
     return (
-        jnp.stack(outputs_list),
-        jnp.stack(input_list),
+        out,
+        grad,
         dense_grad,
         norm_grad,
         expert_grad,

time: 502 us -> 257 us (0.51); the launches traced: 496 us -> 257 us
  Pallas kernels: 50.5 us -> 239 us
  waiting for transfers between devices: 170 us -> 0 us
  matrix products: 105 us -> 0 us
  other arithmetic: 47.3 us -> 0.59 us
  local copies, waits for them, and re-layouts: 54.6 us -> 16.7 us
  starting transfers between devices: 35.3 us -> 0 us
  blocking collectives: 17 us -> 0 us
  between operations: 16 us -> 0.72 us
    pallas_call x0 -> x1, Pallas kernels: none -> 185 us  [block(): pl.pallas_call(partial(block_kernel, cfg), out_shape=(jax.ShapeDtypeStruc...]
    dot_general x40 -> x0, matrix products: 105 us -> none  [the longest x2 35.3 us: shards(): jnp.einsum('rd,fd->rf', rows_in, w_up, preferred_element_type=jnp.float32)]
    all_to_all x8 -> x0, waiting for transfers between devices: 100 us -> none  [the longest x2 36.5 us: shards(): lax.all_to_all(produced.reshape(sources, count, features), 'expert', spli...]
    reduce_scatter x2 -> x0, waiting for transfers between devices: 69.7 us -> none  [the longest x1 53.6 us: shards(): lax.psum_scatter(expert_terms.astype(jnp.bfloat16), 'dp', scatter_dimensi...]
    all_to_all x8 -> x0, starting transfers between devices: 34.8 us -> none  [the longest x2 10 us: shards(): lax.all_to_all(grad_send.reshape(experts, capacity, width), 'expert', spl...]
    reduce_sum x16 -> x1, other arithmetic: 29.9 us -> 0.01 us  [block(): weights = jnp.sum(jnp.where(named, gates[:, 0, None, :, :], 0.0), axis=3)]
    reshape x16 -> x0, local copies, waits for them, and re-layouts: 15.5 us -> none  [the longest x2 2.76 us: shards(): rows_in = received.reshape(sources * count, features)]
    convert_element_type x13 -> x0, other arithmetic: 10.2 us -> none  [the longest x1 2.14 us: shards(): summed_dense, summed_norm, expert_grad = (lax.psum_scatter(grad_dense.ast...]
  transfers between devices with their start and end apart: 14 -> 0, of which waited for: 8 -> 0; matrix products, arithmetic and copies ran while one was open for 28% -> 0% of each run, Pallas kernels for 0% -> 0%
where the time goes in v2:
time: 257 us
  Pallas kernels  239 us (93%)
  local copies, waits for them, and re-layouts  16.7 us (6%)
    pallas_call x1, Pallas kernels, block(): pl.pallas_call(partial(block_kernel, cfg), out_shape=(jax.ShapeDtypeStruc...  185 us
    pallas_call x1, Pallas kernels, muon(): pl.pallas_call(partial(muon_kernel, n_dp, width), out_shape=(full, flat,...  54.5 us
    unnamed x33, local copies, waits for them, and re-layouts  14 us

profile of v2, /device:TPU:5, one launch (start us, length us, event | category | flops | bytes accessed | tf_op | source)
XLA Modules:
  0.0 257.0 jit_solution(6310813798390611830)
XLA Ops:
  0.6 0.0 copy-start.9
  0.7 2.1 copy_bitcast_fusion
  2.8 0.7 copy-done.8
  3.5 0.6 pad.4.weights
  4.1 184.5 %block.1 = (bf16[2,197,512]{2,1,0:T(8,128)(2,1)}, bf16[2,197,512]{2,1,0:T(8,128)(2,1)}, f32[256,512]{1,0:T(8,128)}, f32[4,64]{1,0:T(4,128)}, f32[1,2,256,512]{3,2,1,0:T(8,128)}) custom-call(bf16[2,197,512]{2,1,0:T(8,128)(2,1)} %get-tuple-element.64.images, bf16[2,197,512]{2,1,0:T(8,128)(2,1)} %get-tuple-element.63.cotangent, f32[2,8,256]{2,1,0:T(8,128)} %pad.4.weights, ...), custom_call_target="tpu_custom_call" | custom-call | tf_op jit(solution)/shard_map/block/pallas_call | solution.py:861
  188.6 1.0 copy-done
  189.6 1.0 copy-done.1
  190.7 1.0 copy-done.2
  191.7 54.5 %muon.1 = (f32[1,2,256,512]{3,2,1,0:T(8,128)S(1)}, f32[256,512]{1,0:T(8,128)S(1)}, f32[1,2,256,512]{3,2,1,0:T(8,128)S(1)}, f32[256,512]{1,0:T(8,128)S(1)}, bf16[...) custom-call(f32[1,2,256,512]{3,2,1,0:T(8,128)} %get-tuple-element.82.expert_grad, f32[256,512]{1,0:T(8,128)S(1)} %copy-done, ...), custom_call_target="tpu_custom_call" | custom-call | tf_op jit(solution)/shard_map/muon/pallas_call | solution.py:334
  246.2 0.0 copy-start.7
  246.3 0.7 copy-done.7
  246.9 0.0 copy-done.6
  246.9 0.6 multiply_subtract_fusion
  247.5 1.1 copy.31
  248.6 1.1 copy.32
  249.7 0.8 copy.44
  250.4 0.6 copy.45
  251.0 1.0 copy.46
  252.0 0.8 copy.47
  252.8 1.0 copy.48
  253.8 0.8 copy.49
  254.6 1.0 copy.50
  255.5 0.7 copy.51
  256.2 0.8 copy.52
  (15 shorter events, 0.0 us)
Async XLA Ops:
  0.6 2.1 copy-start.9
  2.8 0.7 copy-start.8
  188.6 1.0 copy-start
  189.6 1.0 copy-start.1
  190.7 1.0 copy-start.2
  191.7 54.5 %copy-start.10 = (f32[4,64]{1,0:T(4,128)S(1)}, f32[4,64]{1,0:T(4,128)}, u32[]{:S(2)}) copy-start(f32[4,64]{1,0:T(4,128)} %param.18) | copy-start | bytes 3076
  191.7 55.8 %copy-start.5 = (bf16[2,197,512]{2,1,0:T(8,128)(2,1)S(1)}, bf16[2,197,512]{2,1,0:T(8,128)(2,1)}, u32[]{:S(2)}) copy-start(bf16[2,197,512]{2,1,0:T(8,128)(2,1)} %get-tuple-element.24) | copy-start | bytes 1210372
  246.2 0.7 copy-start.7
  246.2 0.7 copy-start.6
  247.5 1.1 copy-start.4
  248.6 2.4 copy-start.3

commit v3 on v2

--- a/solution.py
+++ b/solution.py
@@ -396,17 +396,19 @@
 
 
 def block_kernel(
-    cfg, images, cotangent, weights, dense_master, norm_master, expert_master,
-    activations, input_grad, dense_grad, norm_grad, expert_grad,
+    cfg, images, cotangent, gates, routes, dense_master, norm_master, expert_master, dense_momentum, expert_momentum,
+    activations, input_grad, dense_grad, norm_grad, expert_grad, directions,
     dense, experts, norm_slots, norms, tokens, outer_low, normed_low, projected, soft, mixed, residual,
-    rows_x, rows_dy, turned_x, turned_dy, weight_slots, hidden_low, grad_pre_low,
-    produced_sum, grad_in_sum, produced_out, grad_in_out, produced_got, grad_in_got,
+    rows_x, rows_dy, turned_x, turned_dy, weight_slots, hidden_a, hidden_b, grad_pre_a, grad_pre_b, pre_a, pre_b, down_a, down_b,
+    produced_sum, grad_in_sum, produced_out, grad_in_out, produced_mid, grad_in_mid, produced_got, grad_in_got,
     expert_sum, pair_out, pair_got, chip_got, grad_projected, grad_branch,
     dense_sum, dense_out, dense_got, dense_chip, line_out, line_got, line_all, norm_all, norm_line,
+    outgoing, held, directions_got,
     dense_send, dense_take, expert_send, expert_take, norm_send, norm_take,
-    dy_send, dy_take, weight_send, weight_take, x_send, x_take, g_send, g_take, p_send, p_take,
+    dy_send, dy_take, weight_send, weight_take, x_send, x_take, g_send, g_take, gm_send, gm_take, p_send, p_take, pm_send, pm_take,
     pair_send, pair_take, chip_send, chip_take, dpair_send, dpair_take, dchip_send, dchip_take,
     line_send, line_take, lall_send, lall_take, nall_send, nall_take, nline_send, nline_take,
+    row_send, row_take, return_send, return_take,
 ):
     n_dp, n_ex, micro_count, seq, pad, width, heads = cfg
     me, spot = lax.axis_index("dp"), lax.axis_index("expert")
@@ -418,7 +420,8 @@
     shard = expert_master.shape[2]
     dense_shard = dense_master.shape[0]
     norm_shard = norm_master.shape[1]
-    line_rows = n_ex * pad
+    near = n_ex // 2
+    half_rows = near * pad
     head_size = width // heads
     score_scale = head_size ** (-0.5)
 
@@ -433,6 +436,17 @@
 
     def over_ex(step):
         return lax.rem(spot + step, n_ex)
+
+    def mirror(index, distance):
+        other, bit = index, 1
+        while bit <= distance:
+            if distance // bit % 2:
+                other = other + bit - 2 * bit * (index // bit % 2)
+            bit *= 2
+        return other
+
+    def peer(distance):
+        return mirror(spot, distance)
 
     def at_row(ref, index, size):
         return ref.at[pl.ds(pl.multiple_of(index * size, size), size)]
@@ -448,45 +462,69 @@
         at_row(experts.at[job], me, shard)[...] = expert_master[0, job].astype(bf16)
     norm_slots[me] = jnp.zeros(norm_slots.shape[1:], jnp.float32)
     norm_slots[me, 0:4, 0:norm_shard] = norm_master[...].astype(bf16).astype(jnp.float32)
-    weight_slots[spot] = weights[...]
+    expert_row = lax.broadcasted_iota(jnp.int32, (weight_slots.shape[2], seq), 0)
+    for micro in range(micro_count):
+        weight_slots[0, micro] = jnp.zeros(weight_slots.shape[2:], jnp.float32)
+        weight_slots[0, micro, :, 0:seq] = jnp.where(expert_row == routes[micro, 0:1], gates[micro, 0:1], 0.0) + jnp.where(
+            expert_row == routes[micro, 1:2], gates[micro, 1:2], 0.0
+        )
     tail = seq // 16 * 16
     for micro in range(micro_count):
         tokens[micro, tail:] = jnp.zeros((pad - tail, width), bf16)
         tokens[micro, 0:seq] = images[micro]
         outer_low[micro, tail:] = jnp.zeros((pad - tail, width), bf16)
         outer_low[micro, 0:seq] = cotangent[micro]
-        rows_dy[micro, pl.ds(pl.multiple_of(spot * pad, 16), pad)] = outer_low[micro]
-        rows_x[micro, line_rows:] = jnp.zeros((rows_x.shape[1] - line_rows, width), bf16)
-        rows_dy[micro, line_rows:] = jnp.zeros((rows_x.shape[1] - line_rows, width), bf16)
-    hidden_low[line_rows:] = jnp.zeros((rows_x.shape[1] - line_rows, shard), bf16)
-    grad_pre_low[line_rows:] = jnp.zeros((rows_x.shape[1] - line_rows, shard), bf16)
+        rows_dy[micro, 0, 0:pad] = outer_low[micro]
+        for side in range(2):
+            rows_x[micro, side, half_rows:] = jnp.zeros((rows_x.shape[2] - half_rows, width), bf16)
+            rows_dy[micro, side, half_rows:] = jnp.zeros((rows_x.shape[2] - half_rows, width), bf16)
+    for buffer in (hidden_a, hidden_b, grad_pre_a, grad_pre_b):
+        buffer[half_rows:] = jnp.zeros((rows_x.shape[2] - half_rows, shard), bf16)
+    total_rows = held.shape[1]
+    query_devices = 3 * width // dense_shard
+    own_up, own_down, own_query, own_out = 0, 3 * n_dp // 4, n_dp // 4, n_dp // 2
+    dense_owner = jnp.where(me < query_devices, own_query, own_out)
+    dense_place = jnp.where(me < query_devices, me, me - query_devices)
+
+    @pl.when(me == own_query)
+    def _():
+        held[:, 3 * width :] = jnp.zeros((width, total_rows - 3 * width), bf16)
+
+    @pl.when(me == own_out)
+    def _():
+        held[:, n_dp * dense_shard - 3 * width :] = jnp.zeros((width, total_rows - n_dp * dense_shard + 3 * width), bf16)
+
     pl.semaphore_wait(barrier, n_dp + n_ex - 2)
 
-    def gather_copy(views, source, target, send, take):
-        return [copy(view(source), view(source), send.at[k], take.at[k], {"dp": target}) for k, view in enumerate(views)]
+    first_axis, second_axis = 1 + core, 2 - core
+
+    def axis_chip(axis):
+        return jnp.where(axis == 1, mirror(chip, 1), mirror(chip, 2))
+
+    near_chip, next_chip, far_chip = axis_chip(first_axis), axis_chip(second_axis), mirror(chip, 3)
+    sources = [2 * place + core for place in (near_chip, next_chip, far_chip)]
 
     def gather_start(views, send, take):
-        for step in range(0, n_dp, 2):
-            target = over_dp(step) if step else partner
+        for step, target in ((1, sources[0]), (2, sources[1]), (0, partner)):
             for k, view in enumerate(views):
                 copy(view(me), view(me), send.at[k, step], take.at[k, me], {"dp": target}).start()
 
-    def gather_pass(views, send, take):
-        for step in range(2, n_dp, 2):
-            source = lax.rem(me + n_dp - step, n_dp)
+    def gather_got(views, send, take, source):
+        for k, view in enumerate(views):
+            copy(view(source), view(source), send.at[k, 0], take.at[k, source], {"dp": partner}).wait_recv()
+
+    def gather_pass(views, send, take, which):
+        source = sources[which]
+        gather_got(views, send, take, source)
+        for k, view in enumerate(views):
+            if which == 0:
+                copy(view(source), view(source), send.at[k, 3], take.at[k, source], {"dp": sources[1]}).start()
+            copy(view(source), view(source), send.at[k, 4 + which], take.at[k, source], {"dp": partner}).start()
+
+    def gather_sent(views, send, take):
+        for step in range(7):
             for k, view in enumerate(views):
-                copy(view(source), view(source), send.at[k, step], take.at[k, source], {"dp": partner}).wait_recv()
-                copy(view(source), view(source), send.at[k, step + 1], take.at[k, source], {"dp": partner}).start()
-
-    def gather_end(views, send, take):
-        for step in range(0, n_dp, 2):
-            source = lax.rem(partner + n_dp - step, n_dp)
-            for k, view in enumerate(views):
-                copy(view(source), view(source), send.at[k, step], take.at[k, source], {"dp": partner}).wait_recv()
-        for step in range(n_dp):
-            if step != 1:
-                for k, view in enumerate(views):
-                    copy(view(me), view(me), send.at[k, step], take.at[k, me], {"dp": partner}).wait_send()
+                copy(view(me), view(me), send.at[k, step], take.at[k, me], {"dp": partner}).wait_send()
 
     dense_views = [lambda i: at_row(dense, i, dense_shard)]
     expert_views = [lambda i, job=job: at_row(experts.at[job], i, shard) for job in range(2)]
@@ -494,21 +532,34 @@
         copy(norm_slots.at[me], norm_slots.at[me], norm_send.at[step], norm_take.at[me], {"dp": over_dp(step)}).start()
     gather_start(dense_views, dense_send, dense_take)
 
-    def line(ref, micro, index):
-        return ref.at[micro, pl.ds(pl.multiple_of(index * pad, 16), pad)]
-
-    def spread(ref, micro, send, take):
-        for step in range(1, n_ex):
-            copy(line(ref, micro, spot), line(ref, micro, spot), send.at[micro, step], take.at[micro, spot], {"expert": over_ex(step)}).start()
-
-    def spread_end(ref, micro, send, take):
-        for step in range(1, n_ex):
-            source = over_ex(step)
-            copy(line(ref, micro, source), line(ref, micro, source), send.at[micro, step], take.at[micro, source], {"expert": source}).wait()
-
-    for step in range(1, n_ex):
-        copy(weight_slots.at[spot], weight_slots.at[spot], weight_send.at[step], weight_take.at[spot], {"expert": over_ex(step)}).start()
-    spread(rows_dy, 0, dy_send, dy_take)
+    def line(ref, micro, slot):
+        first = slot % near * pad
+        return ref.at[micro, slot // near, first : first + pad]
+
+    def half(ref, micro, side, slot):
+        return ref.at[micro, side, slot * pad : (slot + 1) * pad]
+
+    def spread(ref, micro, send, take, slots):
+        for slot in slots:
+            copy(line(ref, micro, 0), line(ref, micro, slot), send.at[micro, slot], take.at[micro, slot], {"expert": peer(slot)}).start()
+
+    def spread_got(ref, micro, send, take, slot):
+        copy(line(ref, micro, 0), line(ref, micro, slot), send.at[micro, slot], take.at[micro, slot], {"expert": peer(slot)}).wait_recv()
+
+    def spread_pass(ref, micro, send, take):
+        spread_got(ref, micro, send, take, near)
+        for slot in range(1, near):
+            copy(line(ref, micro, near), line(ref, micro, near + slot), send.at[micro, near + slot], take.at[micro, near + slot], {"expert": peer(slot)}).start()
+
+    def spread_sent(ref, micro, send, take, slots):
+        for slot in slots:
+            copy(line(ref, micro, 0), line(ref, micro, slot), send.at[micro, slot], take.at[micro, slot], {"expert": peer(1)}).wait_send()
+
+    near_slots, far_slots = range(1, near), (near,)
+    for slot in range(1, n_ex):
+        copy(weight_slots.at[0], weight_slots.at[slot], weight_send.at[slot], weight_take.at[slot], {"expert": peer(slot)}).start()
+    spread(rows_dy, 0, dy_send, dy_take, far_slots)
+    spread(rows_dy, 0, dy_send, dy_take, near_slots)
 
     for step in range(1, n_dp):
         source = over_dp(step)
@@ -521,12 +572,17 @@
         wide = wide + nn(norm_slots[index].astype(bf16), pick)
     norms[...] = wide
 
-    gather_pass(dense_views, dense_send, dense_take)
+    gather_pass(dense_views, dense_send, dense_take, 0)
+    gather_pass(dense_views, dense_send, dense_take, 1)
+    spread_pass(rows_dy, 0, dy_send, dy_take)
+    spread(rows_dy, 1, dy_send, dy_take, far_slots)
+    gather_pass(dense_views, dense_send, dense_take, 2)
     gather_start(expert_views, expert_send, expert_take)
-    gather_end(dense_views, dense_send, dense_take)
-
-    half = lax.broadcasted_iota(jnp.int32, (pad, 128), 1) < head_size
-    low_masks = [half.astype(jnp.float32).astype(bf16), (1.0 - half.astype(jnp.float32)).astype(bf16)]
+    for place in (chip, mirror(chip, 1), mirror(chip, 2), far_chip):
+        gather_got(dense_views, dense_send, dense_take, 2 * place + 1 - core)
+
+    left = lax.broadcasted_iota(jnp.int32, (pad, 128), 1) < head_size
+    low_masks = [left.astype(jnp.float32).astype(bf16), (1.0 - left.astype(jnp.float32)).astype(bf16)]
     real_key = lax.broadcasted_iota(jnp.int32, (pad, pad), 1) < seq
 
     def pair_of(micro, part, index):
@@ -549,100 +605,209 @@
                 weight = expo / jnp.sum(expo, axis=-1, keepdims=True)
                 soft[micro, 2 * index + side] = weight
                 parts.append(nn(weight.astype(bf16), value))
-            mixed[micro, :, index * 128 : (index + 1) * 128] = jnp.where(half, parts[0], parts[1]).astype(bf16)
+            mixed[micro, :, index * 128 : (index + 1) * 128] = jnp.where(left, parts[0], parts[1]).astype(bf16)
         total = tokens[micro].astype(jnp.float32) + nt(mixed[micro], dense[3 * width :])
         residual[micro] = total
         normed, _ = row_stats(total)
-        line(rows_x, micro, spot)[...] = (normed * norms[2:3] + norms[3:4]).astype(bf16)
-        spread(rows_x, micro, x_send, x_take)
+        rows_x[micro, 0, 0:pad] = (normed * norms[2:3] + norms[3:4]).astype(bf16)
+
+        @pl.when(micro == 0)
+        def _():
+            spread(rows_x, 0, x_send, x_take, near_slots)
+
         return carry
 
     lax.fori_loop(0, micro_count, attend, 0)
-    for micro in range(1, micro_count):
-        spread(rows_dy, micro, dy_send, dy_take)
-    for step in range(1, n_ex):
-        source = over_ex(step)
-        copy(weight_slots.at[source], weight_slots.at[source], weight_send.at[step], weight_take.at[source], {"expert": source}).wait()
-    gather_pass(expert_views, expert_send, expert_take)
-    gather_end(expert_views, expert_send, expert_take)
+    spread(rows_x, 0, x_send, x_take, far_slots)
+    spread_pass(rows_dy, 1, dy_send, dy_take)
+    for slot in range(1, n_ex):
+        copy(weight_slots.at[0], weight_slots.at[slot], weight_send.at[slot], weight_take.at[slot], {"expert": peer(slot)}).wait()
 
     def column_of(slot, micro, row):
         picked = jnp.broadcast_to(weight_slots[slot, micro, pl.ds(row, 1)], (8, weight_slots.shape[3]))
         return picked.T[0:pad, 0:1]
 
-    def send_back(out, got, micro, send, take):
-        for step in range(1, n_ex):
-            target = over_ex(step)
-            copy(line(out, micro, target), line(got, micro, spot), send.at[micro, step], take.at[micro, spot], {"expert": target}).start()
-
-    def send_back_end(out, got, micro, send, take):
-        for step in range(1, n_ex):
-            source = over_ex(step)
-            copy(line(out, micro, source), line(got, micro, source), send.at[micro, step], take.at[micro, source], {"expert": source}).wait()
-
-    for micro in range(micro_count):
-        spread_end(rows_dy, micro, dy_send, dy_take)
-        spread_end(rows_x, micro, x_send, x_take)
-        for block in range(n_ex):
-            where = slice(block * pad, (block + 1) * pad)
-            rows_dy[micro, where] = (column_of(block, micro, spot) * rows_dy[micro, where].astype(jnp.float32)).astype(bf16)
-        turned_x[...] = rows_x[micro].T
-        turned_dy[...] = rows_dy[micro].T
+    def back_near(out, got, micro, send, take):
+        for slot in range(1, near):
+            copy(line(out, micro, slot), got.at[micro, slot - 1], send.at[micro, slot], take.at[micro, slot], {"expert": peer(slot)}).start()
+
+    def back_far(out, mid, micro, send, take):
+        for slot in range(1, near):
+            copy(line(out, micro, near + slot), mid.at[micro, slot - 1], send.at[micro, slot], take.at[micro, slot], {"expert": peer(slot)}).start()
+
+    def back_join(out, mid, got, micro, mid_send, mid_take, send, take):
+        total = line(out, micro, near)[...].astype(jnp.float32)
+        for slot in range(1, near):
+            copy(line(out, micro, near + slot), mid.at[micro, slot - 1], mid_send.at[micro, slot], mid_take.at[micro, slot], {"expert": peer(slot)}).wait()
+            total = total + mid[micro, slot - 1].astype(jnp.float32)
+        line(out, micro, near)[...] = total.astype(bf16)
+        copy(line(out, micro, near), got.at[micro, near - 1], send.at[micro, near], take.at[micro, near], {"expert": peer(near)}).start()
+
+    def back_got(out, got, micro, send, take):
+        total = out[micro, 0, 0:pad].astype(jnp.float32)
+        for slot in range(1, near + 1):
+            where = out.at[micro, 0, 0:pad]
+            copy(where, got.at[micro, slot - 1], send.at[micro, slot], take.at[micro, slot], {"expert": peer(slot)}).wait()
+            total = total + got[micro, slot - 1].astype(jnp.float32)
+        return total
+
+    step_count = 2 * micro_count
+    join_g = lambda micro: back_join(grad_in_out, grad_in_mid, grad_in_got, micro, gm_send, gm_take, g_send, g_take)
+    join_p = lambda micro: back_join(produced_out, produced_mid, produced_got, micro, pm_send, pm_take, p_send, p_take)
+
+    def pair_copy(turn, place):
+        return copy(pair_out.at[lax.rem(turn, 2)], pair_got.at[place], pair_send.at[place], pair_take.at[place], {"dp": partner})
+
+    def chip_step(turn, place):
+        index = 2 * place + core
+        pair_copy(turn, place).wait()
+        for job in range(2):
+            pair_got[place, job] = (expert_sum[index, job] + pair_got[place, job].astype(jnp.float32)).astype(bf16)
+        copy(pair_got.at[place], chip_got.at[chip], chip_send.at[place], chip_take.at[chip], {"dp": index}).start()
+
+    def send_pair(turn, place):
+        pair_out[lax.rem(turn, 2)] = expert_sum[2 * place + 1 - core].astype(bf16)
+        pair_copy(turn, place).start()
+
+    expert_sum[...] = jnp.zeros(expert_sum.shape, jnp.float32)
+
+    def run_step(number, nothing):
+        micro = number // 2
+        side = lax.rem(micro + number, 2)
+        first, last = number == 0, number == step_count - 1
+        for slot in range(1, near):
+            for ref, send, take in ((rows_dy, dy_send, dy_take), (rows_x, x_send, x_take)):
+                copy(half(ref, micro, side, 0), half(ref, micro, side, slot), send.at[micro, slot], take.at[micro, side * near + slot], {"expert": peer(slot)}).wait_recv()
+
+        @pl.when(side == 0)
+        def _():
+            spread_sent(rows_dy, micro, dy_send, dy_take, range(1, near + 1))
+
+        @pl.when(side == 1)
+        def _():
+            spread_sent(rows_dy, micro, dy_send, dy_take, range(near + 1, n_ex))
+
+        @pl.when(first)
+        def _():
+            gather_pass(expert_views, expert_send, expert_take, 0)
+            gather_got(expert_views, expert_send, expert_take, partner)
+
+        gates = [column_of(side * near + slot, micro, spot) for slot in range(near)]
+        for slot in range(near):
+            where = half(rows_dy, micro, side, slot)
+            where[...] = (gates[slot] * where[...].astype(jnp.float32)).astype(bf16)
+        turned_x[...] = rows_x[micro, side].T
+        turned_dy[...] = rows_dy[micro, side].T
         produced_sum[...] = jnp.zeros(produced_sum.shape, jnp.float32)
         grad_in_sum[...] = jnp.zeros(grad_in_sum.shape, jnp.float32)
-        last = micro == micro_count - 1
-
-        def chunk(count, carry, micro=micro, last=last):
-            place = lax.rem(chip + 1 + count // 2, chips)
-            index = 2 * place + lax.rem(count, 2)
-            up = at_row(experts.at[0], index, shard)[...]
-            down = at_row(experts.at[1], index, shard)[...]
-            pre = nt(rows_x[micro, 0:line_rows], up)
-            below, density = gelu_parts(pre)
-            hidden_low[0:line_rows] = (pre * below).astype(bf16)
-            produced_sum[...] += nn(hidden_low[0:line_rows], down)
-            slope = below + pre * density
-            grad_pre_low[0:line_rows] = (nt(rows_dy[micro, 0:line_rows], down) * slope).astype(bf16)
-            grad_in_sum[...] += nn(grad_pre_low[0:line_rows], up)
-            up_grad = nn(turned_x[...], grad_pre_low[...])
-            down_grad = nn(turned_dy[...], hidden_low[...])
-            if micro > 0:
-                up_grad = up_grad + expert_sum[index, 0]
-                down_grad = down_grad + expert_sum[index, 1]
-            expert_sum[index, 0] = up_grad
-            expert_sum[index, 1] = down_grad
-            if last:
-                @pl.when(lax.rem(count, 2) != core)
-                def _():
-                    pair_out[place] = expert_sum[index].astype(bf16)
-                    copy(pair_out.at[place], pair_got.at[place], pair_send.at[place], pair_take.at[place], {"dp": partner}).start()
-
-                @pl.when((lax.rem(count, 2) == 1) & (count >= 3))
-                def _():
-                    chip_step(lax.rem(chip + count // 2, chips))
+
+        def place_of(turn):
+            turn = jnp.where(last, lax.rem(turn + 1, chips), turn)
+            along = jnp.where(
+                turn == 1, jnp.where(last, mirror(chip, 1), near_chip), jnp.where(last, mirror(chip, 2), next_chip)
+            )
+            return jnp.where(turn == 0, chip, jnp.where(turn == 3, far_chip, along))
+
+        def index_of(turn, second):
+            return 2 * place_of(turn) + jnp.where(last, second, lax.rem(core + second, 2))
+
+        def enter(index, pre, down):
+            pre[...] = nt(rows_x[micro, side, 0:half_rows], at_row(experts.at[0], index, shard)[...])
+            down[...] = nt(rows_dy[micro, side, 0:half_rows], at_row(experts.at[1], index, shard)[...])
+
+        def bend(pre, down, hidden, grad_pre):
+            value = pre[...]
+            below, density = gelu_parts(value)
+            hidden[0:half_rows] = (value * below).astype(bf16)
+            grad_pre[0:half_rows] = (down[...] * (below + value * density)).astype(bf16)
+
+        def leave(index, hidden, grad_pre):
+            produced_sum[...] += nn(hidden[0:half_rows], at_row(experts.at[1], index, shard)[...])
+            grad_in_sum[...] += nn(grad_pre[0:half_rows], at_row(experts.at[0], index, shard)[...])
+            expert_sum[index, 0] += nn(turned_x[...], grad_pre[...])
+            expert_sum[index, 1] += nn(turned_dy[...], hidden[...])
+
+        def two_chunks(turn, carry):
+            @pl.when(first & (turn < chips - 2))
+            def _():
+                gather_got(expert_views, expert_send, expert_take, 2 * jnp.where(turn == 0, next_chip, far_chip) + core)
+
+            for step, when, event in events:
+                pl.when((number == step) & (turn == when))(event)
+
+            @pl.when(first)
+            def _():
+                gather_got(expert_views, expert_send, expert_take, 2 * place_of(turn + 1) + 1 - core)
+
+            bend(pre_b, down_b, hidden_b, grad_pre_b)
+            enter(index_of(turn + 1, 0), pre_a, down_a)
+            leave(index_of(turn, 0), hidden_a, grad_pre_a)
+            bend(pre_a, down_a, hidden_a, grad_pre_a)
+            enter(index_of(turn + 1, 1), pre_b, down_b)
+            leave(index_of(turn, 1), hidden_b, grad_pre_b)
+
+            @pl.when(last)
+            def _():
+                send_pair(turn, place_of(turn))
+
+            @pl.when(last & (turn > 0))
+            def _():
+                chip_step(turn - 1, place_of(turn - 1))
             return carry
 
-        def chip_step(place):
-            index = 2 * place + core
-            copy(pair_out.at[place], pair_got.at[place], pair_send.at[place], pair_take.at[place], {"dp": partner}).wait()
-            for job in range(2):
-                pair_got[place, job] = (expert_sum[index, job] + pair_got[place, job].astype(jnp.float32)).astype(bf16)
-            copy(pair_got.at[place], chip_got.at[chip], chip_send.at[place], chip_take.at[chip], {"dp": index}).start()
-
-        lax.fori_loop(0, n_dp, chunk, 0)
-        grad_in_out[micro] = grad_in_sum[...].astype(bf16)
-        send_back(grad_in_out, grad_in_got, micro, g_send, g_take)
-        produced_out[micro] = produced_sum[...].astype(bf16)
-
-    def combine(out, got, micro):
-        line(got, micro, spot)[...] = line(out, micro, spot)[...]
+        def pass_expert(which):
+            source = sources[which]
+            for k, view in enumerate(expert_views):
+                copy(view(source), view(source), expert_send.at[k, 4 + which], expert_take.at[k, source], {"dp": partner}).start()
+
+        events = [
+            (0, 0, partial(pass_expert, 1)),
+            (0, 1, partial(pass_expert, 2)),
+            (0, 1, partial(spread_pass, rows_x, 0, x_send, x_take)),
+            (0, 1, partial(spread, rows_x, 1, x_send, x_take, far_slots)),
+            (1, 0, partial(spread_pass, rows_x, 1, x_send, x_take)),
+            (1, 1, partial(spread, rows_dy, 1, dy_send, dy_take, near_slots)),
+            (1, 1, partial(spread, rows_x, 1, x_send, x_take, near_slots)),
+            (2, 2, partial(join_g, 0)),
+            (3, 1, partial(join_g, 1)),
+        ]
+        enter(index_of(0, 0), pre_a, down_a)
+        bend(pre_a, down_a, hidden_a, grad_pre_a)
+        enter(index_of(0, 1), pre_b, down_b)
+        lax.fori_loop(0, chips - 1, two_chunks, 0)
+        bend(pre_b, down_b, hidden_b, grad_pre_b)
+        leave(index_of(chips - 1, 0), hidden_a, grad_pre_a)
+        leave(index_of(chips - 1, 1), hidden_b, grad_pre_b)
+
+        grad_in_out[micro, side] = grad_in_sum[...].astype(bf16)
+        for slot in range(near):
+            half(produced_out, micro, side, slot)[...] = (gates[slot] * produced_sum[slot * pad : (slot + 1) * pad]).astype(bf16)
+
+        @pl.when(last)
+        def _():
+            send_pair(chips - 1, chip)
+            chip_step(chips - 2, place_of(chips - 2))
+
+        @pl.when(side == 1)
+        def _():
+            back_far(grad_in_out, grad_in_mid, micro, gm_send, gm_take)
+
+        @pl.when(lax.rem(number, 2) == 1)
+        def _():
+            back_near(grad_in_out, grad_in_got, micro, g_send, g_take)
+        return nothing
+
+    lax.fori_loop(0, step_count, run_step, 0)
 
     def attend_back(micro, carry):
-        send_back_end(grad_in_out, grad_in_got, micro, g_send, g_take)
-        combine(grad_in_out, grad_in_got, micro)
-        incoming = jnp.zeros((pad, width), jnp.float32)
-        for index in range(n_ex):
-            incoming = incoming + grad_in_got[micro, index * pad : (index + 1) * pad].astype(jnp.float32)
+        incoming = back_got(grad_in_out, grad_in_got, micro, g_send, g_take)
+
+        @pl.when(micro == micro_count - 1)
+        def _():
+            for index in range(micro_count):
+                back_far(produced_out, produced_mid, index, pm_send, pm_take)
+                back_near(produced_out, produced_got, index, p_send, p_take)
+
         normed, inverse = row_stats(residual[micro])
         gain_two = jnp.sum(incoming * normed, axis=0, keepdims=True)
         bias_two = jnp.sum(incoming, axis=0, keepdims=True)
@@ -668,7 +833,7 @@
             for part in range(3):
                 first = part * width + index * 128
                 grad_projected[pl.ds(pl.multiple_of(micro * pad, 16), pad), first : first + 128] = jnp.where(
-                    half, parts[0][part], parts[1][part]
+                    left, parts[0][part], parts[1][part]
                 ).astype(bf16)
         back = nn(grad_projected[pl.ds(pl.multiple_of(micro * pad, 16), pad)], dense[0 : 3 * width])
         normed, inverse = row_stats(tokens[micro].astype(jnp.float32))
@@ -687,8 +852,6 @@
         grad_branch[micro_count * pad :] = jnp.zeros((depth - micro_count * pad, width), bf16)
     lax.fori_loop(0, micro_count, attend_back, 0)
 
-    for micro in range(micro_count):
-        send_back(produced_out, produced_got, micro, p_send, p_take)
     for step in range(1, n_dp):
         copy(norm_all.at[me], norm_all.at[me], nall_send.at[step], nall_take.at[me], {"dp": over_dp(step)}).start()
 
@@ -729,17 +892,6 @@
         return carry
 
     lax.fori_loop(0, n_dp, dense_chunk, 0)
-
-    copy(pair_out.at[chip], pair_got.at[chip], pair_send.at[chip], pair_take.at[chip], {"dp": partner}).wait()
-    for job in range(2):
-        expert_sum[me, job] = expert_sum[me, job] + pair_got[chip, job].astype(jnp.float32)
-    for step in range(1, chips):
-        place = lax.rem(chip + step, chips)
-        copy(pair_got.at[place], chip_got.at[place], chip_send.at[place], chip_take.at[place], {"dp": 2 * place + core}).wait()
-        for job in range(2):
-            expert_sum[me, job] = expert_sum[me, job] + chip_got[place, job].astype(jnp.float32)
-    for job in range(2):
-        expert_grad[0, job] = expert_sum[me, job].T
 
     copy(dense_out.at[chip], dense_got.at[chip], dpair_send.at[chip], dpair_take.at[chip], {"dp": partner}).wait()
     plane = dense_sum[chip] + dense_got[chip].astype(jnp.float32)
@@ -762,6 +914,35 @@
     norm_line[spot] = norm_total
     for step in range(1, n_ex):
         copy(norm_line.at[spot], norm_line.at[spot], nline_send.at[step], nline_take.at[spot], {"expert": over_ex(step)}).start()
+    pair_copy(chips - 1, chip).wait()
+    for job in range(2):
+        expert_sum[me, job] = expert_sum[me, job] + pair_got[chip, job].astype(jnp.float32)
+    for step in range(1, chips):
+        place = lax.rem(chip + step, chips)
+        copy(pair_got.at[place], chip_got.at[place], chip_send.at[place], chip_take.at[place], {"dp": 2 * place + core}).wait()
+        for job in range(2):
+            expert_sum[me, job] = expert_sum[me, job] + chip_got[place, job].astype(jnp.float32)
+    def slot_of(ref, place, size):
+        return ref.at[:, pl.ds(pl.multiple_of(place * size, size), size)]
+
+    def row_copy(job, owner, place, size):
+        return copy(outgoing.at[job], slot_of(held, place, size), row_send.at[job], row_take.at[me], {"dp": owner})
+
+    def send_rows(job, owner, place, size):
+        @pl.when(me != owner)
+        def _():
+            row_copy(job, owner, place, size).start()
+
+        @pl.when(me == owner)
+        def _():
+            slot_of(held, place, size)[...] = outgoing[job]
+
+    for job, owner in enumerate((own_up, own_down)):
+        outgoing[job] = (DECAY * expert_momentum[0, job].T + expert_sum[me, job]).astype(bf16)
+        send_rows(job, owner, me, shard)
+        expert_grad[0, job] = expert_sum[me, job].T
+    dense_sum[chips] = DECAY * dense_momentum[...].T
+
     summed = line_out[spot].astype(jnp.float32)
     for step in range(1, n_ex):
         source = over_ex(step)
@@ -771,19 +952,95 @@
     for step in range(1, n_ex):
         copy(line_all.at[spot], line_all.at[spot], lall_send.at[step], lall_take.at[spot], {"expert": over_ex(step)}).start()
 
+    for step in range(1, n_ex):
+        source = over_ex(step)
+        copy(line_all.at[source], line_all.at[source], lall_send.at[step], lall_take.at[source], {"expert": source}).wait()
+    for index in range(n_ex):
+        where = slice(index * quarter, (index + 1) * quarter)
+        outgoing[2, where] = (dense_sum[chips, where] + line_all[index].astype(jnp.float32)).astype(bf16)
+    send_rows(2, dense_owner, dense_place, dense_shard)
     for micro in range(micro_count):
-        send_back_end(produced_out, produced_got, micro, p_send, p_take)
-        combine(produced_out, produced_got, micro)
-        total = residual[micro]
-        for index in range(n_ex):
-            gate = weight_slots[spot, micro].T[0:pad, index : index + 1]
-            total = total + gate * produced_got[micro, index * pad : (index + 1) * pad].astype(jnp.float32)
+        join_p(micro)
+
+    gather_sent(dense_views, dense_send, dense_take)
+    gather_sent(expert_views, expert_send, expert_take)
+    for micro in range(micro_count):
+        spread_sent(rows_x, micro, x_send, x_take, range(1, n_ex))
+
+    is_up, is_down, is_query, is_out = me == own_up, me == own_down, me == own_query, me == own_out
+    source_first = jnp.where(is_out, query_devices, 0)
+    source_count = jnp.where(is_query, query_devices, jnp.where(is_out, n_dp - query_devices, n_dp))
+    job_here = jnp.where(is_up, 0, jnp.where(is_down, 1, 2))
+    pieces = total_rows // width
+    halves = width // shard
+
+    def low(piece):
+        return rows_x.at[piece // 2, piece % 2]
+
+    def low_shard(place):
+        first = place % halves * shard
+        return low(place // halves).at[:, first : first + shard]
+
+    blend = turned_x
+
+    def wide(piece, part):
+        return expert_sum.at[piece * halves + part, 0]
+
+    def give(place):
+        target = source_first + place
+
+        @pl.when((place < source_count) & (me != target))
+        def _():
+            copy(low_shard(place), directions_got.at[job_here], return_send.at[place], return_take.at[job_here], {"dp": target}).start()
+
+        @pl.when((place < source_count) & (me == target))
+        def _():
+            directions_got[job_here] = low_shard(place)[...]
+
+    def blend_of(gram):
+        gram_low = gram.astype(bf16)
+        blend[...] = (NS_B * gram + NS_C * nn(gram_low, gram_low)).astype(bf16)
+
+    @pl.when(is_up | is_down | is_query | is_out)
+    def _():
+        for source in range(n_dp):
+            @pl.when((me != source) & (source >= source_first) & (source < source_first + source_count))
+            def _():
+                copy(outgoing.at[0], held.at[:, 0:shard], row_send.at[0], row_take.at[source], {"dp": source}).wait_recv()
+
+        gram = nt(held[...], held[...])
+        same = lax.broadcasted_iota(jnp.int32, (width, width), 0) == lax.broadcasted_iota(jnp.int32, (width, width), 1)
+        trace = jnp.sum(jnp.sum(jnp.where(same, gram, 0.0), axis=0, keepdims=True), axis=1, keepdims=True)
+        scale = 1.0 / (jnp.sqrt(trace) + ORTHO_EPS)
+        blend_of(gram * (scale * scale))
+        for piece in range(pieces):
+            where = slice(piece * width, (piece + 1) * width)
+            part = scale * (NS_A * held[:, where].astype(jnp.float32) + nn(blend[...], held[:, where]))
+            low(piece)[...] = part.astype(bf16)
+            for index in range(halves):
+                wide(piece, index)[...] = part[:, index * shard : (index + 1) * shard]
+
+        def turn(_, carry):
+            every = jnp.concatenate([low(piece)[...] for piece in range(pieces)], axis=1)
+            blend_of(nt(every, every))
+            for piece in range(pieces):
+                part = nn(blend[...], low(piece)[...])
+                for index in range(halves):
+                    fresh = NS_A * wide(piece, index)[...] + part[:, index * shard : (index + 1) * shard]
+                    wide(piece, index)[...] = fresh
+                    low_shard(piece * halves + index)[...] = fresh.astype(bf16)
+            return carry
+
+        lax.fori_loop(0, 4, turn, 0)
+        for place in range(n_dp):
+            give(place)
+
+    for micro in range(micro_count):
+        total = residual[micro] + back_got(produced_out, produced_got, micro, p_send, p_take)
         activations[micro] = total[0:seq].astype(bf16)
-
     for step in range(1, n_ex):
         source = over_ex(step)
         copy(norm_line.at[source], norm_line.at[source], nline_send.at[step], nline_take.at[source], {"expert": source}).wait()
-        copy(line_all.at[source], line_all.at[source], lall_send.at[step], lall_take.at[source], {"expert": source}).wait()
     norm_total = norm_line[0]
     for index in range(1, n_ex):
         norm_total = norm_total + norm_line[index]
@@ -793,22 +1050,76 @@
             norm_grad[...] = norm_total[0:4, index * norm_shard : (index + 1) * norm_shard]
     for index in range(n_ex):
         dense_grad[:, index * quarter : (index + 1) * quarter] = line_all[index].astype(jnp.float32).T
-
-
-def block(images, cotangent, gates, routes, dense_master, norm_master, expert_master):
+    owners = (own_up, own_down, dense_owner)
+    for job, owner in enumerate(owners):
+        @pl.when(me != owner)
+        def _():
+            row_copy(job, owner, 0, shard).wait_send()
+            copy(outgoing.at[job], directions_got.at[job], row_send.at[job], return_take.at[job], {"dp": owner}).wait_recv()
+
+    directions[...] = directions_got[...]
+
+    @pl.when(is_up | is_down | is_query | is_out)
+    def _():
+        for place in range(n_dp):
+            @pl.when((place < source_count) & (me != source_first + place))
+            def _():
+                copy(low_shard(place), directions_got.at[0], return_send.at[place], return_take.at[0], {"dp": source_first + place}).wait_send()
+
+
+def finish_kernel(
+    query_devices, rate, out, grad, dense_grad, norm_grad, expert_grad, directions,
+    dense_momentum, norm_momentum, expert_momentum, dense_master, norm_master, expert_master,
+    out_o, grad_o, dense_grad_o, norm_grad_o, expert_grad_o, dense_moment, norm_moment, expert_moment,
+    dense_new, norm_new, expert_new, dense_copy, expert_copy,
+):
+    for source, target in ((out, out_o), (grad, grad_o), (dense_grad, dense_grad_o), (norm_grad, norm_grad_o), (expert_grad, expert_grad_o)):
+        target[...] = source[...]
+    dense_moment[...] = DECAY * dense_momentum[...] + dense_grad[...]
+    expert_moment[...] = DECAY * expert_momentum[...] + expert_grad[...]
+    moment = DECAY * norm_momentum[...] + norm_grad[...]
+    norm_moment[...] = moment
+    norm_new[...] = norm_master[...] - rate * moment
+    for job in range(2):
+        new = expert_master[0, job] - LR_EXPERT * directions[job].astype(jnp.float32).T
+        expert_new[0, job] = new
+        expert_copy[0, job] = new.astype(jnp.bfloat16)
+    dense_rate = jnp.where(lax.axis_index("dp") < query_devices, LR_QKV, LR_OUT)
+    new = dense_master[...] - dense_rate * directions[2].astype(jnp.float32).T
+    dense_new[...] = new
+    dense_copy[...] = new.astype(jnp.bfloat16)
+
+
+def finish(query_devices, rate, *arrays):
+    out, grad, dense_grad, norm_grad, expert_grad = arrays[:5]
+    f32, bf16 = jnp.float32, jnp.bfloat16
+    shapes = [(out.shape, bf16), (grad.shape, bf16)]
+    trio = [dense_grad.shape, norm_grad.shape, expert_grad.shape]
+    shapes += [(shape, f32) for shape in trio] * 3
+    shapes += [(trio[0], bf16), (trio[2], bf16)]
+    vmem = pl.BlockSpec(memory_space=pltpu.VMEM)
+    return pl.pallas_call(
+        partial(finish_kernel, query_devices, rate),
+        out_shape=tuple(jax.ShapeDtypeStruct(*shape) for shape in shapes),
+        in_specs=[vmem] * len(arrays),
+        out_specs=[vmem] * len(shapes),
+        compiler_params=pltpu.CompilerParams(vmem_limit_bytes=67043328),
+        name="finish",
+    )(*arrays)
+
+
+def block(images, cotangent, gates, routes, dense_master, norm_master, expert_master, dense_momentum, expert_momentum):
     micro_count, _, seq, width = images.shape
     n_dp, n_ex = lax.axis_size("dp"), lax.axis_size("expert")
     pad = -(-seq // 16) * 16
     lanes = -(-seq // 128) * 128
     shard, dense_shard, norm_shard = expert_master.shape[2], dense_master.shape[0], norm_master.shape[1]
     chips = n_dp // 2
-    line_rows = n_ex * pad
-    line_pad = -(-line_rows // 128) * 128
+    near = n_ex // 2
+    half_rows = near * pad
+    half_pad = -(-half_rows // 128) * 128
     slots = -(-n_ex // 8) * 8
     depth = -(-micro_count * pad // 128) * 128
-    named = routes[:, 0, None, :, :] == jnp.arange(slots)[None, :, None, None]
-    weights = jnp.sum(jnp.where(named, gates[:, 0, None, :, :], 0.0), axis=3)
-    weights = jnp.pad(weights, ((0, 0), (0, 0), (0, lanes - seq)))
     vmem = pl.BlockSpec(memory_space=pltpu.VMEM)
     bf16, f32 = jnp.bfloat16, jnp.float32
     dma = pltpu.SemaphoreType.DMA
@@ -825,21 +1136,23 @@
         pltpu.VMEM((micro_count, HEADS, pad, pad), f32),
         pltpu.VMEM(tokens, bf16),
         pltpu.VMEM(tokens, f32),
-        pltpu.VMEM((micro_count, line_pad, width), bf16),
-        pltpu.VMEM((micro_count, line_pad, width), bf16),
-        pltpu.VMEM((width, line_pad), bf16),
-        pltpu.VMEM((width, line_pad), bf16),
+        pltpu.VMEM((micro_count, 2, half_pad, width), bf16),
+        pltpu.VMEM((micro_count, 2, half_pad, width), bf16),
+        pltpu.VMEM((width, half_pad), bf16),
+        pltpu.VMEM((width, half_pad), bf16),
         pltpu.VMEM((n_ex, micro_count, slots, lanes), f32),
-        pltpu.VMEM((line_pad, shard), bf16),
-        pltpu.VMEM((line_pad, shard), bf16),
-        pltpu.VMEM((line_rows, width), f32),
-        pltpu.VMEM((line_rows, width), f32),
-        pltpu.VMEM((micro_count, line_rows, width), bf16),
-        pltpu.VMEM((micro_count, line_rows, width), bf16),
-        pltpu.VMEM((micro_count, line_rows, width), bf16),
-        pltpu.VMEM((micro_count, line_rows, width), bf16),
+        *[pltpu.VMEM((half_pad, shard), bf16)] * 4,
+        *[pltpu.VMEM((half_rows, shard), f32)] * 4,
+        pltpu.VMEM((half_rows, width), f32),
+        pltpu.VMEM((half_rows, width), f32),
+        pltpu.VMEM((micro_count, 2, half_rows, width), bf16),
+        pltpu.VMEM((micro_count, 2, half_rows, width), bf16),
+        pltpu.VMEM((micro_count, near - 1, pad, width), bf16),
+        pltpu.VMEM((micro_count, near - 1, pad, width), bf16),
+        pltpu.VMEM((micro_count, near, pad, width), bf16),
+        pltpu.VMEM((micro_count, near, pad, width), bf16),
         pltpu.VMEM((n_dp, 2, width, shard), f32),
-        pltpu.VMEM((chips, 2, width, shard), bf16),
+        pltpu.VMEM((2, 2, width, shard), bf16),
         pltpu.VMEM((chips, 2, width, shard), bf16),
         pltpu.VMEM((chips, 2, width, shard), bf16),
         pltpu.VMEM((depth, 3 * width), bf16),
@@ -853,10 +1166,14 @@
         pltpu.VMEM((n_ex, width // n_ex, dense_shard), bf16),
         pltpu.VMEM((n_dp, 8, width), f32),
         pltpu.VMEM((n_ex, 8, width), f32),
+        pltpu.VMEM((3, width, shard), bf16),
+        pltpu.VMEM((width, n_dp * shard), bf16),
+        pltpu.VMEM((3, width, shard), bf16),
     ]
     sems = [(1, n_dp), (1, n_dp), (2, n_dp), (2, n_dp), (n_dp,), (n_dp,)]
-    sems += [(micro_count, n_ex)] * 2 + [(n_ex,)] * 2 + [(micro_count, n_ex)] * 6
+    sems += [(micro_count, n_ex)] * 2 + [(n_ex,)] * 2 + [(micro_count, n_ex)] * 10
     sems += [(chips,)] * 8 + [(n_ex,)] * 4 + [(n_dp,)] * 2 + [(n_ex,)] * 2
+    sems += [(3,), (n_dp,), (n_dp,), (3,)]
     cfg = (n_dp, n_ex, micro_count, seq, pad, width, HEADS)
     return pl.pallas_call(
         partial(block_kernel, cfg),
@@ -866,15 +1183,19 @@
             jax.ShapeDtypeStruct(dense_master.shape, f32),
             jax.ShapeDtypeStruct(norm_master.shape, f32),
             jax.ShapeDtypeStruct(expert_master.shape, f32),
+            jax.ShapeDtypeStruct((3, width, shard), bf16),
         ),
-        in_specs=[vmem] * 6,
-        out_specs=[vmem] * 5,
+        in_specs=[vmem] * 9,
+        out_specs=[vmem] * 6,
         scratch_shapes=scratch + [dma(shape) for shape in sems],
         compiler_params=pltpu.CompilerParams(
             collective_id=2, has_side_effects=True, vmem_limit_bytes=67043328
         ),
         name="block",
-    )(images[:, 0], cotangent[:, 0], weights, dense_master, norm_master, expert_master)
+    )(
+        images[:, 0], cotangent[:, 0], gates[:, 0].transpose(0, 2, 1), routes[:, 0].transpose(0, 2, 1),
+        dense_master, norm_master, expert_master, dense_momentum, expert_momentum,
+    )
 
 
 def block_plain(images, cotangent, gates, routes, slots, dense_master, norm_master, expert_master):
@@ -1045,18 +1366,23 @@
     experts = lax.axis_size("expert")
     dp_count = lax.axis_size("dp")
     tokens_all = micro_count * images_here * seq * dp_count * experts
-    lined = dense_master.shape[0] % 128 == 0 and expert_master.shape[2] % 128 == 0
-    if lined and images_here == 1 and dp_count % 2 == 0 and width == 64 * HEADS:
-        out, grad, dense_grad, norm_grad, expert_grad = block(
-            images, cotangent, gates, routes, dense_master, norm_master, expert_master
-        )
-        out, grad = out[:, None], grad[:, None]
-    else:
-        out, grad, dense_grad, norm_grad, expert_grad = block_plain(
-            images, cotangent, gates, routes, slots, dense_master, norm_master, expert_master
-        )
+    lined = dense_master.shape[0] % 128 == 0 and expert_master.shape[2] % 128 == 0 and experts in (4, 8)
+    lined = lined and dense_master.shape[0] == expert_master.shape[2] and micro_count == 2 and dp_count == 8
+    vector_rate = LR_VECTOR * tokens_all ** (-0.5)
+    if lined and images_here == 1 and width == 64 * HEADS:
+        arrays = block(
+            images, cotangent, gates, routes, dense_master, norm_master, expert_master, dense_momentum, expert_momentum
+        )
+        out, grad, *rest = finish(
+            3 * width // dense_master.shape[0], vector_rate, *arrays,
+            dense_momentum, norm_momentum, expert_momentum, dense_master, norm_master, expert_master,
+        )
+        return (out[:, None], grad[:, None], *rest)
+    out, grad, dense_grad, norm_grad, expert_grad = block_plain(
+        images, cotangent, gates, routes, slots, dense_master, norm_master, expert_master
+    )
     norm_moment = DECAY * norm_momentum + norm_grad
-    norm_new = norm_master - LR_VECTOR * tokens_all ** (-0.5) * norm_moment
+    norm_new = norm_master - vector_rate * norm_moment
     expert_moment, dense_moment, expert_new, dense_new, expert_copy, dense_copy = muon(
         expert_grad, dense_grad, expert_momentum, dense_momentum, expert_master, dense_master
     )

time: 257 us -> 202 us (0.79); the launches traced: 257 us -> 199 us
  Pallas kernels: 239 us -> 193 us
  local copies, waits for them, and re-layouts: 16.7 us -> 5.27 us
    pallas_call x1, Pallas kernels: 54.5 us -> 5.88 us  [finish(): pl.pallas_call(partial(finish_kernel, query_devices, rate), out_shape=tup...]
    unnamed x33 -> x4, local copies, waits for them, and re-layouts: 14 us -> 3.18 us
where the time goes in v3:
time: 202 us; the launch traced here: 199 us
  Pallas kernels  193 us (96%)
  local copies, waits for them, and re-layouts  5.27 us (3%)
    pallas_call x1, Pallas kernels, block(): pl.pallas_call(partial(block_kernel, cfg), out_shape=(jax.ShapeDtypeStruc...  187 us
    pallas_call x1, Pallas kernels, finish(): pl.pallas_call(partial(finish_kernel, query_devices, rate), out_shape=tup...  5.88 us

profile of v3, /device:TPU:5, one launch (start us, length us, event | category | flops | bytes accessed | tf_op | source)
XLA Modules:
  0.0 198.7 jit_solution(2629742816900561730)
XLA Ops:
  0.6 2.1 %copy_bitcast_fusion = (bf16[2,197,512]{2,1,0:T(8,128)(2,1)}, bf16[2,197,512]{2,1,0:T(8,128)(2,1)}) fusion(bf16[2,1,197,512]{3,0,2,1:T(2,128)(2,1)} %param.12, bf16[2,1,197,512]{3,0,2,1:T(2,128)(2,1)} %param.11), kind=kLoop, calls=%fused_computation | loop fusion | bytes 1613824 | tf_op jit(solution)/shard_map/squeeze | solution.py:1196
  2.7 186.9 %block.1 = (bf16[2,197,512]{2,1,0:T(8,128)(2,1)}, bf16[2,197,512]{2,1,0:T(8,128)(2,1)}, f32[256,512]{1,0:T(8,128)}, f32[4,64]{1,0:T(4,128)}, f32[1,2,256,512]{3,2,1,0:T(8,128)}, /*index=5*/bf16[3,512,256]{2,1,0:T(8,128)(2,1)}) custom-call(bf16[2,197,512]{2,1,0:T(8,128)(2,1)} %get-tuple-element.65.images, bf16[2,197,512]{2,1,0:T(8,128)(2,1)} %get-tuple-element.64.cotangent, ...), custom_call_target="tpu_custom_call" | custom-call | tf_op jit(solution)/shard_map/block/pallas_call | solution.py:1178
  189.6 5.9 %finish.1 = (bf16[2,197,512]{2,1,0:T(8,128)(2,1)}, bf16[2,197,512]{2,1,0:T(8,128)(2,1)}, f32[256,512]{1,0:T(8,128)}, f32[4,64]{1,0:T(4,128)}, f32[1,2,256,512]{3...) custom-call(bf16[2,197,512]{2,1,0:T(8,128)(2,1)} %get-tuple-element., ...), custom_call_target="tpu_custom_call" | custom-call | tf_op jit(solution)/shard_map/finish/pallas_call | solution.py:1101
  195.5 0.0 copy-start
  195.5 2.1 %copy.25 = bf16[2,1,197,512]{3,0,2,1:T(2,128)(2,1)} copy(bf16[2,1,197,512]{3,2,0,1:T(8,128)(2,1)} %bitcast.13) | data formatting | bytes 806912
  197.6 0.0 copy-done
  197.6 1.1 copy.26
Async XLA Ops:
  195.5 2.1 %copy-start = (bf16[2,197,512]{2,1,0:T(8,128)(2,1)S(1)}, bf16[2,197,512]{2,1,0:T(8,128)(2,1)}, u32[]{:S(2)}) copy-start(bf16[2,197,512]{2,1,0:T(8,128)(2,1)} %get-tuple-element.39) | copy-start | bytes 1210372
